TPU v7x, 8 devices: a whole 2x2x1 slice. The times are simulated.
8 devices in a mesh: data: 1 (over z), tp: 2 (over y), ep: 4 (over x, core).
Axes of the slice: x: 2, y: 2, z: 1, core: 2. Of those that a mesh axis runs over, the one named last changes fastest.
Arguments:
- tokens_a: bfloat16 [2048, 1280], P(('data', 'ep', 'tp'))
- tokens_b: bfloat16 [2048, 1280], P(('data', 'ep', 'tp'))
- experts_a: int32 [2048, 6], P(('data', 'ep', 'tp'))
- experts_b: int32 [2048, 6], P(('data', 'ep', 'tp'))
- gates_a: float32 [2048, 6], P(('data', 'ep', 'tp'))
- gates_b: float32 [2048, 6], P(('data', 'ep', 'tp'))
- slots_a: int32 [2048, 6], P(('data', 'ep', 'tp'))
- slots_b: int32 [2048, 6], P(('data', 'ep', 'tp'))
- shared_w1: bfloat16 [1280, 1792], P(None, 'tp')
- shared_w3: bfloat16 [1280, 1792], P(None, 'tp')
- shared_w2: bfloat16 [1792, 1280], P('tp')
- routed_w1: bfloat16 [64, 1280, 896], P('ep')
- routed_w3: bfloat16 [64, 1280, 896], P('ep')
- routed_w2: bfloat16 [64, 896, 1280], P('ep')
Outputs:
- output 1: bfloat16 [2048, 1280], P(('data', 'ep', 'tp'))
- output 2: bfloat16 [2048, 1280], P(('data', 'ep', 'tp'))
All inputs are finite; a program needn't handle non-finite values.
Results may differ from a plain program's by a relative error of at most 0.00608049.
Values are sent between devices in bfloat16 or wider.
A program may use at most 1 GiB of HBM per device.

v0:
```python
import jax
import jax.numpy as jnp
from jax import lax
from jax.sharding import PartitionSpec as P


def capacity_rows(tok_local, top_k, num_experts):
    return max(4, (2 * tok_local * top_k) // num_experts)


def swiglu_rows(rows, w_in, w_gate, w_out):
    proj_in = jnp.dot(rows, w_in, preferred_element_type=jnp.float32)
    proj_gate = jnp.dot(rows, w_gate, preferred_element_type=jnp.float32)
    hidden = (jax.nn.silu(proj_in) * proj_gate).astype(jnp.bfloat16)
    return jnp.dot(hidden, w_out, preferred_element_type=jnp.float32)


def solution(mesh):
    ep_size = mesh.shape['ep']
    tok_spec = P(('data', 'ep', 'tp'), None)
    in_specs = (tok_spec,) * 8 + (P(None, 'tp'), P(None, 'tp'), P('tp', None), P('ep', None, None), P('ep', None, None), P('ep', None, None))

    def shared_path(x_local, shared_w1, shared_w3, shared_w2):
        gathered = lax.all_gather(x_local, 'tp', axis=0, tiled=True)
        partial_sum = swiglu_rows(gathered, shared_w1, shared_w3, shared_w2)
        return lax.psum_scatter(partial_sum, 'tp', scatter_dimension=0, tiled=True)

    def routed_path(x_local, expert_ids, gate_vals, slot_ids, routed_w1, routed_w3, routed_w2):
        tok_local, top_k = expert_ids.shape
        local_experts, model_dim, expert_ff = routed_w1.shape
        cap_rows = capacity_rows(tok_local, top_k, local_experts * ep_size)
        num_rows = local_experts * ep_size * cap_rows
        dest_rank = expert_ids // local_experts
        local_id = expert_ids % local_experts
        keep_mask = slot_ids >= 0
        row_ids = jnp.where(keep_mask, (local_id * ep_size + dest_rank) * cap_rows + slot_ids, -1)
        place_mat = jnp.any(row_ids[:, :, None] == jnp.arange(num_rows)[None, None, :], axis=1).astype(jnp.bfloat16)
        send_rows = jnp.einsum('tr,td->rd', place_mat, x_local, preferred_element_type=jnp.float32).astype(jnp.bfloat16)
        recv_rows = lax.all_to_all(send_rows.reshape(local_experts, ep_size, cap_rows, model_dim), 'ep', 1, 1, tiled=True)
        recv_rows = recv_rows.reshape(local_experts, ep_size * cap_rows, model_dim)
        proj_in = jnp.einsum('erd,edf->erf', recv_rows, routed_w1, preferred_element_type=jnp.float32)
        proj_gate = jnp.einsum('erd,edf->erf', recv_rows, routed_w3, preferred_element_type=jnp.float32)
        hidden = (jax.nn.silu(proj_in) * proj_gate).astype(jnp.bfloat16)
        expert_out = jnp.einsum('erf,efd->erd', hidden, routed_w2, preferred_element_type=jnp.float32).astype(jnp.bfloat16)
        back_rows = lax.all_to_all(expert_out.reshape(local_experts, ep_size, cap_rows, model_dim), 'ep', 1, 1, tiled=True)
        picked = jnp.take(back_rows.reshape(num_rows, model_dim), jnp.maximum(row_ids, 0), axis=0)
        weights = jnp.where(keep_mask, gate_vals, 0.0)
        return jnp.sum(picked.astype(jnp.float32) * weights[:, :, None], axis=1)

    def layer_local(tokens_a, tokens_b, experts_a, experts_b, gates_a, gates_b, slots_a, slots_b, shared_w1, shared_w3, shared_w2, routed_w1, routed_w3, routed_w2):
        def one_microbatch(x_local, expert_ids, gate_vals, slot_ids):
            shared_out = shared_path(x_local, shared_w1, shared_w3, shared_w2)
            routed_out = routed_path(x_local, expert_ids, gate_vals, slot_ids, routed_w1, routed_w3, routed_w2)
            return (x_local.astype(jnp.float32) + shared_out + routed_out).astype(jnp.bfloat16)
        out_a = one_microbatch(tokens_a, experts_a, gates_a, slots_a)
        out_b = one_microbatch(tokens_b, experts_b, gates_b, slots_b)
        return (out_a, out_b)

    return jax.shard_map(layer_local, mesh=mesh, in_specs=in_specs, out_specs=(tok_spec, tok_spec), check_vma=False)
```

profile of v0, /device:TPU:0, one launch (start us, length us, event | category | flops | bytes accessed | tf_op | source)
XLA Modules:
  0.0 454.2 jit_solution(16388320987669206201)
XLA Ops:
  13.5 7.0 %convolution_convert_fusion = bf16[3072,1280]{1,0:T(8,128)(2,1)} fusion(pred[256,3072]{1,0:T(8,128)(4,1)S(1)} %fusion.1, bf16[256,1280]{1,0:T(8,128)(2,1)} %param.17), kind=kOutput, calls=%fused_computation.6 | convolution fusion | flops 2017198080 | bytes 9306112 | tf_op jit(solution)/shard_map/tr,td->rd/dot_general | solution.py:38
  20.5 7.1 %copy.54 = bf16[16,4,48,1280]{3,2,0,1:T(8,128)(2,1)} copy(bf16[16,4,48,1280]{3,2,1,0:T(8,128)(2,1)} %bitcast.34) | data formatting | bytes 15728640 | tf_op jit(solution)/shard_map/reshape | solution.py:39
  27.6 5.7 %all-to-all-start.2 = ((bf16[16,4,48,1280]{3,2,0,1:T(8,128)(2,1)}), bf16[16,4,48,1280]{3,2,0,1:T(8,128)(2,1)}, u32[]{:S(2)}, u32[]{:S(2)}) async-start(bf16[16,4,48,1280]{3,2,0,1:T(8,128)(2,1)} %copy.54), calls=%async_computation.4 | async-start | bytes 15728640 | tf_op jit(solution)/shard_map/all_to_all | solution.py:39
  40.8 6.0 %convolution_convert_fusion.1 = bf16[3072,1280]{1,0:T(8,128)(2,1)} fusion(pred[256,3072]{1,0:T(8,128)(4,1)S(1)} %fusion, bf16[256,1280]{1,0:T(8,128)(2,1)S(1)} %copy-done.3), kind=kOutput, calls=%fused_computation.7 | convolution fusion | flops 2017198080 | bytes 9306112 | tf_op jit(solution)/shard_map/tr,td->rd/dot_general | solution.py:38
  46.8 7.1 %copy.47 = bf16[16,4,48,1280]{3,2,0,1:T(8,128)(2,1)} copy(bf16[16,4,48,1280]{3,2,1,0:T(8,128)(2,1)} %bitcast.35) | data formatting | bytes 15728640 | tf_op jit(solution)/shard_map/reshape | solution.py:39
  53.9 6.2 %all-gather.5.cloned.1.call-done = bf16[512,1280]{1,0:T(8,128)(2,1)} async-done(((bf16[256,1280]{1,0:T(8,128)(2,1)}), bf16[512,1280]{1,0:T(8,128)(2,1)}) %all-gather.5.cloned.1.call-update) | async-done | bytes 1310736 | tf_op jit(solution)/shard_map/all_gather | solution.py:24
  64.9 7.1 %fusion.9 = f32[512,1280]{1,0:T(8,128)} fusion(bf16[896,1280]{1,0:T(8,128)(2,1)S(1)} %copy-done, f32[512,896]{1,0:T(8,128)} %fusion.36, bf16[512,1280]{1,0:T(8,128)(2,1)} %all-gather.5.cloned.1.call-done, bf16[1280,896]{1,0:T(8,128)(2,1)} %param.25), kind=kOutput, calls=%fused_computation.23 | convolution fusion | flops 2351562752 | bytes 10354688 | tf_op jit(solution)/shard_map/dot_general | solution.py:15
  72.1 49.4 %all-to-all-done.2 = bf16[16,4,48,1280]{3,2,0,1:T(8,128)(2,1)} async-done(((bf16[16,4,48,1280]{3,2,0,1:T(8,128)(2,1)}), bf16[16,4,48,1280]{3,2,0,1:T(8,128)(2,1)}, u32[]{:S(2)}, u32[]{:S(2)}) %all-to-all-start.2) | async-done | bytes 7864352 | tf_op jit(solution)/shard_map/all_to_all | solution.py:39
  121.5 5.7 %all-to-all-start = ((bf16[16,4,48,1280]{3,2,0,1:T(8,128)(2,1)}), bf16[16,4,48,1280]{3,2,0,1:T(8,128)(2,1)}, u32[]{:S(2)}, u32[]{:S(2)}) async-start(bf16[16,4,48,1280]{3,2,0,1:T(8,128)(2,1)} %copy.47), calls=%async_computation.1 | async-start | bytes 15728640 | tf_op jit(solution)/shard_map/all_to_all | solution.py:39
  127.2 7.2 %copy.55 = bf16[16,4,48,1280]{3,2,1,0:T(8,128)(2,1)} copy(bf16[16,4,48,1280]{3,2,0,1:T(8,128)(2,1)} %all-to-all-done.2) | data formatting | bytes 15728640 | tf_op jit(solution)/shard_map/all_to_all | solution.py:39
  134.4 22.5 %fusion.37 = f32[16,192,896]{2,1,0:T(8,128)} fusion(bf16[16,192,1280]{2,1,0:T(8,128)(2,1)} %bitcast.36, bf16[16,1280,896]{2,1,0:T(8,128)(2,1)} %param.27), kind=kOutput, calls=%fused_computation.71 | convolution fusion | flops 7046430720 | bytes 55574528 | tf_op jit(solution)/shard_map/erd,edf->erf/dot_general | solution.py:41
  156.9 35.3 %convolution_convert_fusion.2 = bf16[16,192,1280]{2,1,0:T(8,128)(2,1)} fusion(bf16[16,896,1280]{2,1,0:T(8,128)(2,1)} %param.29, f32[16,192,896]{2,1,0:T(8,128)} %fusion.37, bf16[16,192,1280]{2,1,0:T(8,128)(2,1)} %bitcast.37, bf16[16,1280,896]{2,1,0:T(8,128)(2,1)} %param.28), kind=kOutput, calls=%fused_computation.12 | convolution fusion | flops 14113308672 | bytes 100139008 | tf_op jit(solution)/shard_map/erf,efd->erd/dot_general | solution.py:44
  192.1 7.0 %copy.56 = bf16[16,4,48,1280]{3,2,0,1:T(8,128)(2,1)} copy(bf16[16,4,48,1280]{3,2,1,0:T(8,128)(2,1)} %bitcast.40) | data formatting | bytes 15728640 | tf_op jit(solution)/shard_map/reshape | solution.py:45
  199.2 15.2 %all-to-all-done = bf16[16,4,48,1280]{3,2,0,1:T(8,128)(2,1)} async-done(((bf16[16,4,48,1280]{3,2,0,1:T(8,128)(2,1)}), bf16[16,4,48,1280]{3,2,0,1:T(8,128)(2,1)}, u32[]{:S(2)}, u32[]{:S(2)}) %all-to-all-start) | async-done | bytes 7864352 | tf_op jit(solution)/shard_map/all_to_all | solution.py:39
  214.4 5.8 %all-to-all-start.3 = ((bf16[16,4,48,1280]{3,2,0,1:T(8,128)(2,1)}), bf16[16,4,48,1280]{3,2,0,1:T(8,128)(2,1)}, u32[]{:S(2)}, u32[]{:S(2)}) async-start(bf16[16,4,48,1280]{3,2,0,1:T(8,128)(2,1)} %copy.56), calls=%async_computation.5 | async-start | bytes 15728640 | tf_op jit(solution)/shard_map/all_to_all | solution.py:45
  220.2 7.2 %copy.48 = bf16[16,4,48,1280]{3,2,1,0:T(8,128)(2,1)} copy(bf16[16,4,48,1280]{3,2,0,1:T(8,128)(2,1)} %all-to-all-done) | data formatting | bytes 15728640 | tf_op jit(solution)/shard_map/all_to_all | solution.py:39
  227.4 22.5 %fusion.35 = f32[16,192,896]{2,1,0:T(8,128)} fusion(bf16[16,192,1280]{2,1,0:T(8,128)(2,1)} %bitcast.38, bf16[16,1280,896]{2,1,0:T(8,128)(2,1)} %param.27), kind=kOutput, calls=%fused_computation.69 | convolution fusion | flops 7046430720 | bytes 55574528 | tf_op jit(solution)/shard_map/erd,edf->erf/dot_general | solution.py:41
  249.8 35.3 %convolution_convert_fusion.3 = bf16[16,192,1280]{2,1,0:T(8,128)(2,1)} fusion(bf16[16,896,1280]{2,1,0:T(8,128)(2,1)} %param.29, f32[16,192,896]{2,1,0:T(8,128)} %fusion.35, bf16[16,192,1280]{2,1,0:T(8,128)(2,1)} %bitcast.39, bf16[16,1280,896]{2,1,0:T(8,128)(2,1)} %param.28), kind=kOutput, calls=%fused_computation.13 | convolution fusion | flops 14113308672 | bytes 100139008 | tf_op jit(solution)/shard_map/erf,efd->erd/dot_general | solution.py:44
  285.1 7.0 %copy.49 = bf16[16,4,48,1280]{3,2,0,1:T(8,128)(2,1)} copy(bf16[16,4,48,1280]{3,2,1,0:T(8,128)(2,1)} %bitcast.41) | data formatting | bytes 15728640 | tf_op jit(solution)/shard_map/reshape | solution.py:45
  292.1 15.3 %all-to-all-done.3 = bf16[16,4,48,1280]{3,2,0,1:T(8,128)(2,1)} async-done(((bf16[16,4,48,1280]{3,2,0,1:T(8,128)(2,1)}), bf16[16,4,48,1280]{3,2,0,1:T(8,128)(2,1)}, u32[]{:S(2)}, u32[]{:S(2)}) %all-to-all-start.3) | async-done | bytes 7864352 | tf_op jit(solution)/shard_map/all_to_all | solution.py:45
  307.4 5.5 %all-to-all-start.1 = ((bf16[16,4,48,1280]{3,2,0,1:T(8,128)(2,1)}), bf16[16,4,48,1280]{3,2,0,1:T(8,128)(2,1)}, u32[]{:S(2)}, u32[]{:S(2)}) async-start(bf16[16,4,48,1280]{3,2,0,1:T(8,128)(2,1)} %copy.49), calls=%async_computation.2 | async-start | bytes 15728640 | tf_op jit(solution)/shard_map/all_to_all | solution.py:45
  313.2 4.9 %fusion.34 = f32[512,896]{1,0:T(8,128)} fusion(bf16[512,1280]{1,0:T(8,128)(2,1)} %all-gather.3.cloned.1.call-done, bf16[1280,896]{1,0:T(8,128)(2,1)} %param.24), kind=kOutput, calls=%fused_computation.68 | convolution fusion | flops 1174405120 | bytes 5439488 | tf_op jit(solution)/shard_map/dot_general | solution.py:12
  318.2 7.2 %fusion.8 = f32[512,1280]{1,0:T(8,128)} fusion(bf16[896,1280]{1,0:T(8,128)(2,1)S(1)} %copy-done, f32[512,896]{1,0:T(8,128)} %fusion.34, bf16[512,1280]{1,0:T(8,128)(2,1)} %all-gather.3.cloned.1.call-done, bf16[1280,896]{1,0:T(8,128)(2,1)} %param.25), kind=kOutput, calls=%fused_computation.22 | convolution fusion | flops 2351562752 | bytes 10354688 | tf_op jit(solution)/shard_map/dot_general | solution.py:15
  326.8 7.2 %copy.57 = bf16[16,4,48,1280]{3,2,1,0:T(8,128)(2,1)} copy(bf16[16,4,48,1280]{3,2,0,1:T(8,128)(2,1)} %all-to-all-done.3) | data formatting | bytes 15728640 | tf_op jit(solution)/shard_map/all_to_all | solution.py:45
  334.0 13.5 %gather_fusion.1 = bf16[1536,1280]{1,0:T(8,128)(2,1)} fusion(bf16[3072,1280]{1,0:T(8,128)(2,1)} %bitcast.32, s32[2048]{0:T(1024)S(1)} %pad_clamp_fusion), kind=kCustom, calls=%fused_computation.1.clone | custom fusion | bytes 7870464 | tf_op jit(solution)/shard_map/jit(_take)/gather | solution.py:46
  347.5 7.1 %reshape.72 = bf16[256,6,1280]{2,1,0:T(8,128)(2,1)} reshape(bf16[1536,1280]{1,0:T(8,128)(2,1)} %gather_fusion.1) | data formatting | bytes 7864320 | tf_op jit(solution)/shard_map/jit(_take)/gather | solution.py:46
  354.6 45.5 %all-to-all-done.1 = bf16[16,4,48,1280]{3,2,0,1:T(8,128)(2,1)} async-done(((bf16[16,4,48,1280]{3,2,0,1:T(8,128)(2,1)}), bf16[16,4,48,1280]{3,2,0,1:T(8,128)(2,1)}, u32[]{:S(2)}, u32[]{:S(2)}) %all-to-all-start.1) | async-done | bytes 7864352 | tf_op jit(solution)/shard_map/all_to_all | solution.py:45
  400.1 7.1 %copy.50 = bf16[16,4,48,1280]{3,2,1,0:T(8,128)(2,1)} copy(bf16[16,4,48,1280]{3,2,0,1:T(8,128)(2,1)} %all-to-all-done.1) | data formatting | bytes 15728640 | tf_op jit(solution)/shard_map/all_to_all | solution.py:45
  407.3 13.2 %gather_fusion = bf16[1536,1280]{1,0:T(8,128)(2,1)} fusion(bf16[3072,1280]{1,0:T(8,128)(2,1)} %bitcast.33, s32[2048]{0:T(1024)S(1)} %pad_clamp_fusion.1), kind=kCustom, calls=%fused_computation.clone | custom fusion | bytes 7870464 | tf_op jit(solution)/shard_map/jit(_take)/gather | solution.py:46
  420.5 7.1 %reshape.68 = bf16[256,6,1280]{2,1,0:T(8,128)(2,1)} reshape(bf16[1536,1280]{1,0:T(8,128)(2,1)} %gather_fusion) | data formatting | bytes 7864320 | tf_op jit(solution)/shard_map/jit(_take)/gather | solution.py:46
  427.6 7.9 %multiply_reduce_fusion = f32[256,1280]{1,0:T(8,128)} fusion(bf16[256,6,1280]{2,1,0:T(8,128)(2,1)} %reshape.72, f32[256,6]{1,0:T(8,128)S(1)} %copy.59, pred[256,6]{1,0:T(8,128)(4,1)S(1)} %copy.53), kind=kLoop, calls=%fused_computation.10 | loop fusion | flops 7536640 | bytes 5250560 | tf_op jit(solution)/shard_map/reduce_sum | solution.py:48
  435.5 6.0 %multiply_reduce_fusion.1 = f32[256,1280]{1,0:T(8,128)} fusion(bf16[256,6,1280]{2,1,0:T(8,128)(2,1)S(1)} %copy-done.1, f32[256,6]{1,0:T(8,128)S(1)} %copy.52, pred[256,6]{1,0:T(8,128)(4,1)S(1)} %copy.46), kind=kLoop, calls=%fused_computation.11 | loop fusion | flops 7536640 | bytes 5250560 | tf_op jit(solution)/shard_map/reduce_sum | solution.py:48
  (64 shorter events, 25.9 us)
Async XLA Ops:
  7.2 57.8 %copy-start = (bf16[896,1280]{1,0:T(8,128)(2,1)S(1)}, bf16[896,1280]{1,0:T(8,128)(2,1)}, u32[]{:S(2)}) copy-start(bf16[896,1280]{1,0:T(8,128)(2,1)} %param.26) | copy-start | bytes 6881284
  8.7 0.6 copy-start.4
  27.6 7.7 %copy-start.9 = (s32[256,6]{0,1:T(8,128)S(1)}, s32[256,6]{0,1:T(8,128)}, u32[]{:S(2)}) copy-start(s32[256,6]{0,1:T(8,128)} %param.22) | copy-start | bytes 18436
  27.6 7.8 %copy-start.13 = (s32[256,6]{0,1:T(8,128)S(1)}, s32[256,6]{0,1:T(8,128)}, u32[]{:S(2)}) copy-start(s32[256,6]{0,1:T(8,128)} %param.18) | copy-start | bytes 18436
  27.6 13.2 %copy-start.3 = (bf16[256,1280]{1,0:T(8,128)(2,1)S(1)}, bf16[256,1280]{1,0:T(8,128)(2,1)}, u32[]{:S(2)}) copy-start(bf16[256,1280]{1,0:T(8,128)(2,1)} %param.16) | copy-start | bytes 1966084
  27.6 93.9 %all-to-all-start.2 = ((bf16[16,4,48,1280]{3,2,0,1:T(8,128)(2,1)}), bf16[16,4,48,1280]{3,2,0,1:T(8,128)(2,1)}, u32[]{:S(2)}, u32[]{:S(2)}) async-start(bf16[16,4,48,1280]{3,2,0,1:T(8,128)(2,1)} %copy.54), calls=%async_computation.4 | async-start | bytes 15728640 | tf_op jit(solution)/shard_map/all_to_all | solution.py:39
  33.3 26.8 %all-gather.5.cloned.1.call-start = ((), (), s32[]{:S(2)}) async-start(), calls=%async_computation.8 | async-start | bytes 1966080 | tf_op jit(solution)/shard_map/all_gather | solution.py:24
  34.0 279.2 %all-gather.3.cloned.1.call-start = ((), (), s32[]{:S(2)}) async-start(), calls=%async_computation.6 | async-start | bytes 1966080 | tf_op jit(solution)/shard_map/all_gather | solution.py:24
  34.8 406.7 %reduce-scatter.5.cloned.1.call-start = ((), (), s32[]{:S(2)}) async-start(), calls=%async_computation.9 | async-start | bytes 3932160 | tf_op jit(solution)/shard_map/reduce_scatter | solution.py:26
  36.0 0.6 copy-start.6
  121.5 92.9 %all-to-all-start = ((bf16[16,4,48,1280]{3,2,0,1:T(8,128)(2,1)}), bf16[16,4,48,1280]{3,2,0,1:T(8,128)(2,1)}, u32[]{:S(2)}, u32[]{:S(2)}) async-start(bf16[16,4,48,1280]{3,2,0,1:T(8,128)(2,1)} %copy.47), calls=%async_computation.1 | async-start | bytes 15728640 | tf_op jit(solution)/shard_map/all_to_all | solution.py:39
  214.4 93.0 %all-to-all-start.3 = ((bf16[16,4,48,1280]{3,2,0,1:T(8,128)(2,1)}), bf16[16,4,48,1280]{3,2,0,1:T(8,128)(2,1)}, u32[]{:S(2)}, u32[]{:S(2)}) async-start(bf16[16,4,48,1280]{3,2,0,1:T(8,128)(2,1)} %copy.56), calls=%async_computation.5 | async-start | bytes 15728640 | tf_op jit(solution)/shard_map/all_to_all | solution.py:45
  307.4 92.7 %all-to-all-start.1 = ((bf16[16,4,48,1280]{3,2,0,1:T(8,128)(2,1)}), bf16[16,4,48,1280]{3,2,0,1:T(8,128)(2,1)}, u32[]{:S(2)}, u32[]{:S(2)}) async-start(bf16[16,4,48,1280]{3,2,0,1:T(8,128)(2,1)} %copy.49), calls=%async_computation.2 | async-start | bytes 15728640 | tf_op jit(solution)/shard_map/all_to_all | solution.py:45
  312.9 131.3 %reduce-scatter.3.cloned.1.call-start = ((), (), s32[]{:S(2)}) async-start(), calls=%async_computation.7 | async-start | bytes 3932160 | tf_op jit(solution)/shard_map/reduce_scatter | solution.py:26
  318.1 7.2 %copy-start.5 = (s32[256,6]{0,1:T(8,128)S(1)}, s32[256,6]{0,1:T(8,128)}, u32[]{:S(2)}) copy-start(s32[256,6]{0,1:T(8,128)} %copy-done.4) | copy-start | bytes 18436
  318.1 7.5 %copy-start.14 = (pred[256,6]{0,1:T(8,128)(4,1)S(1)}, pred[256,6]{0,1:T(8,128)(4,1)}, u32[]{:S(2)}) copy-start(pred[256,6]{0,1:T(8,128)(4,1)} %get-tuple-element.3) | copy-start | bytes 4612
  318.1 7.7 %copy-start.8 = (s32[256,6]{0,1:T(8,128)S(1)}, s32[256,6]{0,1:T(8,128)}, u32[]{:S(2)}) copy-start(s32[256,6]{0,1:T(8,128)} %param.23) | copy-start | bytes 18436
  318.1 7.7 %copy-start.11 = (f32[256,6]{0,1:T(8,128)S(1)}, f32[256,6]{0,1:T(8,128)}, u32[]{:S(2)}) copy-start(f32[256,6]{0,1:T(8,128)} %param.21) | copy-start | bytes 18436
  318.2 7.9 %copy-start.7 = (s32[256,6]{0,1:T(8,128)S(1)}, s32[256,6]{0,1:T(8,128)}, u32[]{:S(2)}) copy-start(s32[256,6]{0,1:T(8,128)} %copy-done.6) | copy-start | bytes 18436
  318.2 8.2 %copy-start.15 = (pred[256,6]{0,1:T(8,128)(4,1)S(1)}, pred[256,6]{0,1:T(8,128)(4,1)}, u32[]{:S(2)}) copy-start(pred[256,6]{0,1:T(8,128)(4,1)} %get-tuple-element.5) | copy-start | bytes 4612
  318.2 8.4 %copy-start.10 = (s32[256,6]{0,1:T(8,128)S(1)}, s32[256,6]{0,1:T(8,128)}, u32[]{:S(2)}) copy-start(s32[256,6]{0,1:T(8,128)} %param.22) | copy-start | bytes 18436
  318.2 8.4 %copy-start.12 = (f32[256,6]{0,1:T(8,128)S(1)}, f32[256,6]{0,1:T(8,128)}, u32[]{:S(2)}) copy-start(f32[256,6]{0,1:T(8,128)} %param.20) | copy-start | bytes 18436
  427.6 7.9 %copy-start.1 = (bf16[256,6,1280]{2,1,0:T(8,128)(2,1)S(1)}, bf16[256,6,1280]{2,1,0:T(8,128)(2,1)}, u32[]{:S(2)}) copy-start(bf16[256,6,1280]{2,1,0:T(8,128)(2,1)} %reshape.68) | copy-start | bytes 11796484
  427.6 13.9 %copy-start.2 = (bf16[256,1280]{1,0:T(8,128)(2,1)S(1)}, bf16[256,1280]{1,0:T(8,128)(2,1)}, u32[]{:S(2)}) copy-start(bf16[256,1280]{1,0:T(8,128)(2,1)} %param.17) | copy-start | bytes 1966084
Sparse Core Ops, SparseCore 0:
  35.6 24.4 all-gather.4
  61.6 21.1 all-gather.2
  84.9 34.7 reduce-scatter.4
  325.5 37.0 reduce-scatter.2
where the time goes:
time: 461 us; the launch traced here: 454 us
  matrix products  152 us (33%)
  waiting for transfers between devices  133 us (29%)
  local copies, waits for them, and re-layouts  100 us (22%)
  other arithmetic  30.1 us (7%)
  starting transfers between devices  23.6 us (5%)
  between operations  14.6 us (3%)
    dot_general x2, matrix products, routed_path(): jnp.einsum('erf,efd->erd', hidden, routed_w2, preferred_element_type=jnp....  70.5 us
    all_to_all x2, waiting for transfers between devices, routed_path(): lax.all_to_all(send_rows.reshape(local_experts, ep_size, cap_rows, model_...  64.6 us
    all_to_all x2, waiting for transfers between devices, routed_path(): lax.all_to_all(expert_out.reshape(local_experts, ep_size, cap_rows, model...  60.8 us
    dot_general x2, matrix products, routed_path(): jnp.einsum('erd,edf->erf', recv_rows, routed_w1, preferred_element_type=j...  45 us
    gather x4, local copies, waits for them, and re-layouts, routed_path(): jnp.take(back_rows.reshape(num_rows, model_dim), jnp.maximum(row_ids, 0),...  41 us
    all_to_all x2, local copies, waits for them, and re-layouts, routed_path(): lax.all_to_all(send_rows.reshape(local_experts, ep_size, cap_rows, model_...  14.4 us
    all_to_all x2, local copies, waits for them, and re-layouts, routed_path(): lax.all_to_all(expert_out.reshape(local_experts, ep_size, cap_rows, model...  14.3 us
    dot_general x2, matrix products, swiglu_rows(): return jnp.dot(hidden, w_out, preferred_element_type=jnp.float32)  14.3 us
  transfers between devices with their start and end apart: 8, of which 5 were waited for; matrix products, arithmetic and copies ran while one was open for 57% of the time, Pallas kernels for 0%

commit v1 on v0

v1 whole, which is shorter than its diff:
```python
import functools

import jax
import jax.numpy as jnp
from jax import lax
from jax.experimental import pallas as pl
from jax.experimental.pallas import tpu as pltpu
from jax.sharding import PartitionSpec as P

MESH = pl.DeviceIdType.MESH
BF16 = jnp.bfloat16
F32 = jnp.float32

TOK = 256
D = 1280
F = 896
TOP_K = 6
CAP = 48
EXP = 16
NSRC = 4
GRP = 4
COL = 256
NCOL = D // COL
ROWS = NSRC * CAP
SLOTS13 = 3


def dot(a, b):
    return jnp.dot(a, b, preferred_element_type=F32)


def kernel(xa, xb, meta, sw1, sw3, sw2, rw1, rw3, rw2,
           oa, ob, pw1, pw3, pw2,
           metabuf, tokbuf, slots, gmat, rowsg, hbuf, ybuf, hs, send1, send3, tmp0, tmp2, q0, q2, rr, w13, w2b,
           meta_s, meta_r, tc_s, tc_r, tx_s, tx_r, td_s, td_r, p1_s, p1_r, p3_s, p3_r, rr_s, rr_r,
           yw_s, yw_r, fw_s, fw_r, w13_s, w2_s, sw2_s):
    ep = lax.axis_index("ep")
    tp = lax.axis_index("tp")
    core = lax.rem(ep, 2)
    core_peer = {"ep": ep + 1 - 2 * core}
    x_peer = {"ep": lax.rem(ep + 2, 4)}
    diag = {"ep": 3 - ep}
    y_peer = {"tp": 1 - tp}
    own = (xa, xb)

    def remote(src, dst, s, r, dev):
        return pltpu.make_async_remote_copy(src_ref=src, dst_ref=dst, send_sem=s, recv_sem=r, device_id=dev, device_id_type=MESH)

    def w13_copies(u):
        slot = lax.rem(u, SLOTS13)
        e = lax.rem(u, EXP)
        return (pltpu.make_async_copy(rw1.at[e], w13.at[slot, 0], w13_s.at[slot, 0]),
                pltpu.make_async_copy(rw3.at[e], w13.at[slot, 1], w13_s.at[slot, 1]))

    def w2_copy(step, q):
        n = lax.rem(step, NCOL)
        return pltpu.make_async_copy(rw2.at[pl.ds(q * GRP, GRP), :, pl.ds(pl.multiple_of(n * COL, COL), COL)], w2b.at[q], w2_s.at[q])

    for u in range(SLOTS13):
        for cp in w13_copies(u):
            cp.start()

    barrier = pltpu.get_barrier_semaphore()
    for dev in (core_peer, x_peer, diag, y_peer):
        pl.semaphore_signal(barrier, inc=1, device_id=dev, device_id_type=MESH)
    pl.semaphore_wait(barrier, 4)

    meta_cp = [remote(meta, metabuf.at[i], meta_s.at[i], meta_r.at[i], dev) for i, dev in enumerate((core_peer, x_peer, diag))]
    x_cp = [remote(own[m], tokbuf.at[m, 1], tx_s.at[m], tx_r.at[m], x_peer) for m in range(2)]
    c_cp = [remote(own[m], tokbuf.at[m, 0], tc_s.at[m], tc_r.at[m], core_peer) for m in range(2)]
    d_cp = [remote(tokbuf.at[m, 1], tokbuf.at[m, 2], td_s.at[m], td_r.at[m], core_peer) for m in range(2)]
    for cp in meta_cp:
        cp.start()
    x_cp[0].start()
    c_cp[0].start()
    c_cp[1].start()

    half_d, half_f = D // 2, F // 2
    rows_d = pl.ds(pl.multiple_of(core * half_d, 128), half_d)
    rows_f = pl.ds(pl.multiple_of(core * half_f, 64), half_f)
    yw_cp = [remote(w.at[r], p.at[r], yw_s.at[i], yw_r.at[i], y_peer)
             for i, (w, p, r) in enumerate(((sw1, pw1, rows_d), (sw3, pw3, rows_d), (sw2, pw2, rows_f)))]
    fw_cp = [remote(p.at[r], p.at[r], fw_s.at[i], fw_r.at[i], core_peer)
             for i, (p, r) in enumerate(((pw1, rows_d), (pw3, rows_d), (pw2, rows_f)))]
    for cp in yw_cp:
        cp.start()
    for q in range(EXP // GRP):
        w2_copy(0, q).start()

    for cp in meta_cp:
        cp.wait()

    def route(i, carry):
        m, src = i // NSRC, lax.rem(i, NSRC)
        info = jnp.where(src == 0, meta[m], metabuf[lax.max(src, 1) - 1, m])
        first = ((ep * EXP + lax.broadcasted_iota(jnp.int32, (EXP, TOK), 0)) * CAP).astype(F32)
        slot = jnp.full((EXP, TOK), -1.0, F32)
        gate = jnp.zeros((EXP, TOK), F32)
        for j in range(TOP_K):
            s = info[j:j + 1, :] - first
            hit = (s >= 0.0) & (s < float(CAP))
            slot = jnp.where(hit, s, slot)
            gate = jnp.where(hit, info[TOP_K + j:TOP_K + j + 1, :], gate)
        pos = lax.broadcasted_iota(jnp.int32, (CAP, TOK), 0).astype(F32)
        for e in range(EXP):
            slots[m, src, e] = slot[e:e + 1, :]
        part = EXP // 2
        for k in range(2):
            g = jnp.concatenate([jnp.where(pos == slot[e:e + 1, :], gate[e:e + 1, :], 0.0)
                                 for e in range(k * part, (k + 1) * part)], axis=0).T
            hi = g.astype(BF16)
            g = g - hi.astype(F32)
            mid = g.astype(BF16)
            low = (g - mid.astype(F32)).astype(BF16)
            for p, v in enumerate((hi, mid, low)):
                gmat[m, src, :, pl.ds(p * EXP * CAP + k * part * CAP, part * CAP)] = v
        return carry

    lax.fori_loop(0, 2 * NSRC, route, 0)

    def arrive(m):
        c_cp[m].wait()
        x_cp[m].wait()
        d_cp[m].start()

    def swiglu_in(x, w1, w3, store):
        full = F // COL
        for k in range(full):
            cols = pl.ds(k * COL, COL)
            a = dot(x, w1[:, cols])
            b = dot(x, w3[:, cols])
            store(cols, (jax.nn.silu(a) * b).astype(BF16))
        cols = pl.ds(full * COL, F - full * COL)
        ab = dot(x, jnp.concatenate([w1[:, cols], w3[:, cols]], axis=1))
        a, b = ab[:, :F - full * COL], ab[:, F - full * COL:]
        store(cols, (jax.nn.silu(a) * b).astype(BF16))

    def phase1(m):
        toks = (own[m], tokbuf.at[m, 0], tokbuf.at[m, 1], tokbuf.at[m, 2])

        def group(g, carry):
            pos = lax.broadcasted_iota(jnp.int32, (CAP, TOK), 0).astype(F32)
            for src in range(NSRC):
                place = jnp.concatenate([jnp.where(pos == slots[m, src, g * GRP + i], 1.0, 0.0) for i in range(GRP)], axis=0).astype(BF16)
                for n in range(NCOL):
                    cols = pl.ds(n * COL, COL)
                    r = dot(place, toks[src][:, cols]).astype(BF16)
                    for i in range(GRP):
                        rowsg[i, pl.ds(src * CAP, CAP), cols] = r[i * CAP:(i + 1) * CAP]

            def expert(i, carry):
                u = m * EXP + g * GRP + i
                slot = lax.rem(u, SLOTS13)
                for cp in w13_copies(u):
                    cp.wait()
                e = g * GRP + i

                def store(cols, v):
                    hbuf[e, :, cols] = v

                swiglu_in(rowsg[i], w13.at[slot, 0], w13.at[slot, 1], store)

                @pl.when(u + SLOTS13 < 2 * EXP)
                def _():
                    for cp in w13_copies(u + SLOTS13):
                        cp.start()
                return carry

            return lax.fori_loop(0, GRP, expert, carry)

        lax.fori_loop(0, EXP // GRP, group, 0)

    def sum_copies(step, m=None):
        par = lax.rem(step, 2)
        return (remote(send1.at[par], q0.at[step], p1_s.at[step], p1_r.at[step], core_peer),
                remote(send3.at[par], q2.at[step], p3_s.at[step], p3_r.at[step], core_peer),
                remote(q2.at[step], rr.at[step], rr_s.at[step], rr_r.at[step], x_peer))

    def phase2(m):
        def column(n, carry):
            step = m * NCOL + n
            par = lax.rem(step, 2)
            for q in range(EXP // GRP):
                w2_copy(step, q).wait()
                for i in range(GRP):
                    e = q * GRP + i
                    y = dot(hbuf[e], w2b[q, i]).astype(BF16)
                    for src in range(NSRC):
                        ybuf[src, e] = y[src * CAP:(src + 1) * CAP]

                @pl.when(step + 1 < 2 * NCOL)
                def _():
                    w2_copy(step + 1, q).start()

            def combine(src):
                y = ybuf[src].reshape(EXP * CAP, COL)
                k = EXP * CAP
                g = gmat.at[m, src]
                return dot(g[:, :k], y) + dot(g[:, k:2 * k], y) + dot(g[:, 2 * k:], y)

            @pl.when(step >= 2)
            def _():
                old1, old3, _unused = sum_copies(step - 2)
                old1.wait_send()
                old3.wait_send()

            cp1, cp3, cpr = sum_copies(step)
            send3[par] = combine(3)
            cp3.start()
            tmp2[...] = combine(2)
            send1[par] = combine(1)
            cp1.start()
            tmp0[...] = combine(0)
            cp3.wait_recv()
            q2[step] = q2[step] + tmp2[...]
            cpr.start()
            cp1.wait_recv()
            q0[step] = q0[step] + tmp0[...]
            return carry

        lax.fori_loop(0, NCOL, column, 0)

    arrive(0)
    x_cp[1].start()
    d_cp[0].wait()
    phase1(0)
    arrive(1)
    phase2(0)
    d_cp[1].wait()
    phase1(1)

    local13 = (pltpu.make_async_copy(sw1, w13.at[2, 0], w13_s.at[2, 0]), pltpu.make_async_copy(sw3, w13.at[2, 1], w13_s.at[2, 1]))
    peer13 = (pltpu.make_async_copy(pw1, w13.at[0, 0], w13_s.at[0, 0]), pltpu.make_async_copy(pw3, w13.at[0, 1], w13_s.at[0, 1]))
    for cp in local13:
        cp.start()
    for i in range(2):
        yw_cp[i].wait()
        fw_cp[i].start()
    phase2(1)
    for i in range(2):
        fw_cp[i].wait()
        peer13[i].start()
    yw_cp[2].wait()
    fw_cp[2].start()

    def shared_in(half, slot):
        for m in range(2):
            def store(cols, v):
                hs[half, pl.ds(m * TOK, TOK), cols] = v

            swiglu_in(own[m][...], w13.at[slot, 0], w13.at[slot, 1], store)

    for cp in local13:
        cp.wait()
    shared_in(0, 2)
    fw_cp[2].wait()

    def sw2_copies(n):
        cols = pl.ds(n * COL, COL)
        slot = n % GRP
        return (pltpu.make_async_copy(sw2.at[:, cols], w2b.at[slot, 0], sw2_s.at[slot, 0]),
                pltpu.make_async_copy(pw2.at[:, cols], w2b.at[slot, 1], sw2_s.at[slot, 1]))

    for n in range(GRP):
        for cp in sw2_copies(n):
            cp.start()
    for cp in peer13:
        cp.wait()
    shared_in(1, 0)
    for n in range(NCOL):
        for cp in sw2_copies(n):
            cp.wait()
        cols = pl.ds(n * COL, COL)
        for m in range(2):
            rows = pl.ds(m * TOK, TOK)
            s = dot(hs[0, rows, :], w2b[n % GRP, 0]) + dot(hs[1, rows, :], w2b[n % GRP, 1])
            q0[m * NCOL + n] = q0[m * NCOL + n] + s + own[m][:, cols].astype(F32)
        if n + GRP < NCOL:
            for cp in sw2_copies(n + GRP):
                cp.start()
    for m, out in enumerate((oa, ob)):
        for n in range(NCOL):
            step = m * NCOL + n
            sum_copies(step)[2].wait()
            out[:, pl.ds(n * COL, COL)] = (q0[step] + rr[step]).astype(BF16)
    for step in range(2 * NCOL - 2, 2 * NCOL):
        cp1, cp3, _unused = sum_copies(step)
        cp1.wait_send()
        cp3.wait_send()


def solution(mesh):
    tok_spec = P(('data', 'ep', 'tp'), None)
    in_specs = (tok_spec,) * 8 + (P(None, 'tp'), P(None, 'tp'), P('tp', None), P('ep', None, None), P('ep', None, None), P('ep', None, None))

    def layer_local(tokens_a, tokens_b, experts_a, experts_b, gates_a, gates_b, slots_a, slots_b,
                    shared_w1, shared_w3, shared_w2, routed_w1, routed_w3, routed_w2):
        def info(experts, gates, slots):
            row = jnp.where(slots >= 0, experts * CAP + slots, -1).astype(F32)
            return jnp.concatenate([row.T, gates.T], axis=0)

        meta = jnp.stack([info(experts_a, gates_a, slots_a), info(experts_b, gates_b, slots_b)])
        vmem = pl.BlockSpec(memory_space=pltpu.VMEM)
        hbm = pl.BlockSpec(memory_space=pltpu.HBM)
        sem = pltpu.SemaphoreType.DMA
        steps = 2 * NCOL
        out = pl.pallas_call(
            kernel,
            name="moe_layer",
            out_shape=(jax.ShapeDtypeStruct((TOK, D), BF16), jax.ShapeDtypeStruct((TOK, D), BF16),
                       jax.ShapeDtypeStruct((D, F), BF16), jax.ShapeDtypeStruct((D, F), BF16), jax.ShapeDtypeStruct((F, D), BF16)),
            in_specs=[vmem] * 3 + [hbm] * 6,
            out_specs=(vmem, vmem, hbm, hbm, hbm),
            scratch_shapes=[
                pltpu.VMEM((3, 2, 2 * TOP_K, TOK), F32),
                pltpu.VMEM((2, 3, TOK, D), BF16),
                pltpu.VMEM((2, NSRC, EXP, 1, TOK), F32),
                pltpu.VMEM((2, NSRC, TOK, 3 * EXP * CAP), BF16),
                pltpu.VMEM((GRP, ROWS, D), BF16),
                pltpu.VMEM((EXP, ROWS, F), BF16),
                pltpu.VMEM((NSRC, EXP, CAP, COL), BF16),
                pltpu.VMEM((2, 2 * TOK, F), BF16),
                pltpu.VMEM((2, TOK, COL), F32),
                pltpu.VMEM((2, TOK, COL), F32),
                pltpu.VMEM((TOK, COL), F32),
                pltpu.VMEM((TOK, COL), F32),
                pltpu.VMEM((steps, TOK, COL), F32),
                pltpu.VMEM((steps, TOK, COL), F32),
                pltpu.VMEM((steps, TOK, COL), F32),
                pltpu.VMEM((SLOTS13, 2, D, F), BF16),
                pltpu.VMEM((EXP // GRP, GRP, F, COL), BF16),
                sem((3,)), sem((3,)), sem((2,)), sem((2,)), sem((2,)), sem((2,)), sem((2,)), sem((2,)),
                sem((steps,)), sem((steps,)), sem((steps,)), sem((steps,)), sem((steps,)), sem((steps,)),
                sem((3,)), sem((3,)), sem((3,)), sem((3,)), sem((SLOTS13, 2)), sem((EXP // GRP,)), sem((EXP // GRP, 2)),
            ],
            compiler_params=pltpu.CompilerParams(collective_id=0, has_side_effects=True, vmem_limit_bytes=67043328),
        )(tokens_a, tokens_b, meta, shared_w1, shared_w3, shared_w2, routed_w1, routed_w3, routed_w2)
        return out[0], out[1]

    return jax.shard_map(layer_local, mesh=mesh, in_specs=in_specs, out_specs=(tok_spec, tok_spec), check_vma=False)
```

time: 461 us -> 136 us (0.30); the launches traced: 454 us -> 136 us
  matrix products: 152 us -> 0 us
  waiting for transfers between devices: 133 us -> 0 us
  Pallas kernels: 0 us -> 129 us
  local copies, waits for them, and re-layouts: 100 us -> 3.93 us
  other arithmetic: 30.1 us -> 2.79 us
  starting transfers between devices: 23.6 us -> 0 us
  between operations: 14.6 us -> 0.64 us
    dot_general x10 -> x0, matrix products: 152 us -> none  [the longest x2 70.5 us: routed_path(): jnp.einsum('erf,efd->erd', hidden, routed_w2, preferred_element_type=jnp....]
    pallas_call x0 -> x1, Pallas kernels: none -> 129 us  [layer_local(): pl.pallas_call(kernel, name='moe_layer', out_shape=(jax.ShapeDtypeStruct(...]
    all_to_all x4 -> x0, waiting for transfers between devices: 125 us -> none  [the longest x2 64.6 us: routed_path(): lax.all_to_all(send_rows.reshape(local_experts, ep_size, cap_rows, model_...]
    gather x4 -> x0, local copies, waits for them, and re-layouts: 41 us -> none  [routed_path(): jnp.take(back_rows.reshape(num_rows, model_dim), jnp.maximum(row_ids, 0),...]
    all_to_all x4 -> x0, local copies, waits for them, and re-layouts: 28.7 us -> none  [the longest x2 14.4 us: routed_path(): lax.all_to_all(send_rows.reshape(local_experts, ep_size, cap_rows, model_...]
    reshape x4 -> x0, local copies, waits for them, and re-layouts: 28.3 us -> none  [the longest x2 14.2 us: routed_path(): send_rows.reshape(local_experts, ep_size, cap_rows, model_dim)]
    all_to_all x4 -> x0, starting transfers between devices: 22.7 us -> none  [the longest x2 11.4 us: routed_path(): lax.all_to_all(send_rows.reshape(local_experts, ep_size, cap_rows, model_...]
    reduce_sum x2 -> x0, other arithmetic: 13.9 us -> none  [routed_path(): return jnp.sum(picked.astype(jnp.float32) * weights[:, :, None], axis=1)]
  transfers between devices with their start and end apart: 8 -> 0, of which waited for: 5 -> 0; matrix products, arithmetic and copies ran while one was open for 57% -> 0% of each run, Pallas kernels for 0% -> 0%
where the time goes in v1:
time: 136 us
  Pallas kernels  129 us (95%)
  local copies, waits for them, and re-layouts  3.93 us (3%)
  other arithmetic  2.79 us (2%)
    pallas_call x1, Pallas kernels, layer_local(): pl.pallas_call(kernel, name='moe_layer', out_shape=(jax.ShapeDtypeStruct(...  129 us
    unnamed x2, local copies, waits for them, and re-layouts  3.93 us

profile of v1, /device:TPU:0, one launch (start us, length us, event | category | flops | bytes accessed | tf_op | source)
XLA Modules:
  0.0 136.1 jit_solution(9680488220490853828)
XLA Ops:
  0.6 0.7 convert_bitcast_fusion.1
  1.4 0.7 convert_bitcast_fusion
  2.1 0.7 maximum_bitcast_fusion
  2.8 0.6 pad_maximum_fusion.meta
  3.4 128.7 %moe_layer.1 = (bf16[256,1280]{1,0:T(8,128)(2,1)}, bf16[256,1280]{1,0:T(8,128)(2,1)}, bf16[1280,896]{1,0:T(8,128)(2,1)}, bf16[1280,896]{1,0:T(8,128)(2,1)}, bf16[896,1280]{1,0:T(8,128)(2,1)}) custom-call(bf16[256,1280]{1,0:T(8,128)(2,1)} %xa.1, bf16[256,1280]{1,0:T(8,128)(2,1)} %xb.1, f32[2,12,256]{2,1,0:T(8,128)} %pad_maximum_fusion.meta, ...), custom_call_target="tpu_custom_call" | custom-call | tf_op jit(solution)/shard_map/moe_layer/pallas_call | solution.py:307
  132.2 2.0 %copy.18 = bf16[256,1280]{1,0:T(8,128)(2,1)} copy(bf16[256,1280]{1,0:T(8,128)(2,1)} %get-tuple-element.10) | data formatting | bytes 1310720
  134.1 2.0 %copy.19 = bf16[256,1280]{1,0:T(8,128)(2,1)} copy(bf16[256,1280]{1,0:T(8,128)(2,1)} %get-tuple-element.11) | data formatting | bytes 1310720

commit v2 on v1

v2 whole, which is shorter than its diff:
```python
import functools

import jax
import jax.numpy as jnp
from jax import lax
from jax.experimental import pallas as pl
from jax.experimental.pallas import tpu as pltpu
from jax.sharding import PartitionSpec as P

MESH = pl.DeviceIdType.MESH
BF16 = jnp.bfloat16
F32 = jnp.float32

TOK = 256
D = 1280
F = 896
TOP_K = 6
CAP = 48
EXP = 16
NSRC = 4
XP, DG, OWN, CP = range(NSRC)
GRP = 4
COL = 256
NCOL = D // COL
ROWS = NSRC * CAP
SIDE = 2 * CAP
SLOTS13 = 4
SLOTS2 = 3
HALF = EXP // 2


def dot(a, b):
    return jnp.dot(a, b, preferred_element_type=F32)


def kernel(xa, xb, ea, eb, ga, gb, sa, sb, sw1, sw3, sw2, rw1, rw3, rw2,
           oa, ob, pw1, pw3, pw2,
           ids, gates, tokbuf, slots, gmat, rowsg, hs, hfar, hnear, ybuf, send, tmp, q0, q2, rr, w13, w2b,
           own_s, meta_s, meta_r, fmeta_s, fmeta_r, tc_s, tc_r, tx_s, tx_r, td_s, td_r, p1_s, p1_r, p3_s, p3_r, rr_s, rr_r,
           yw_s, yw_r, fw_s, fw_r, w13_s, w2_s, sw2_s, out_s):
    ep = lax.axis_index("ep")
    tp = lax.axis_index("tp")
    core = lax.rem(ep, 2)
    core_peer = {"ep": ep + 1 - 2 * core}
    x_peer = {"ep": lax.rem(ep + 2, 4)}
    diag = {"ep": 3 - ep}
    y_peer = {"tp": 1 - tp}
    own = (xa, xb)

    def remote(src, dst, s, r, dev):
        return pltpu.make_async_remote_copy(src_ref=src, dst_ref=dst, send_sem=s, recv_sem=r, device_id=dev, device_id_type=MESH)

    def expert_of(u):
        return lax.rem(jnp.where(u < EXP, u, u + EXP - SLOTS13), EXP)

    def w13_copies(u):
        slot = lax.rem(u, SLOTS13)
        e = expert_of(u)
        return (pltpu.make_async_copy(rw1.at[e], w13.at[slot, 0], w13_s.at[slot, 0]),
                pltpu.make_async_copy(rw3.at[e], w13.at[slot, 1], w13_s.at[slot, 1]))

    def w2_copy(unit):
        slot = lax.rem(unit, SLOTS2)
        n = lax.rem(lax.div(unit, 2), NCOL)
        first = lax.rem(unit, 2) * HALF
        return pltpu.make_async_copy(rw2.at[pl.ds(first, HALF), :, pl.ds(pl.multiple_of(n * COL, COL), COL)], w2b.at[slot], w2_s.at[slot])

    routing = ((ea, sa, ga), (eb, sb, gb))

    def routing_slots(m, src):
        return ids.at[src, m, 0], ids.at[src, m, 1], gates.at[src, m]

    own_cp = [pltpu.make_async_copy(a, b, own_s.at[m, k]) for m in range(2)
              for k, (a, b) in enumerate(zip((*routing[m], own[m]), (*routing_slots(m, OWN), tokbuf.at[m, OWN])))]
    for cp in own_cp:
        cp.start()

    barrier = pltpu.get_barrier_semaphore()
    for dev in (core_peer, x_peer, diag, y_peer):
        pl.semaphore_signal(barrier, inc=1, device_id=dev, device_id_type=MESH)
    pl.semaphore_wait(barrier, 4)

    def routing_cp(m, k, src, dst, ss, rs, dev):
        return remote(src[k], routing_slots(m, dst)[k], ss.at[m, k], rs.at[m, k], dev)

    cmeta_cp = [[routing_cp(m, k, routing[m], CP, meta_s.at[0], meta_r.at[0], core_peer) for k in range(3)] for m in range(2)]
    xmeta_cp = [[routing_cp(m, k, routing[m], XP, meta_s.at[1], meta_r.at[1], x_peer) for k in range(3)] for m in range(2)]
    dmeta_cp = [[routing_cp(m, k, routing_slots(m, XP), DG, fmeta_s, fmeta_r, core_peer) for k in range(3)] for m in range(2)]
    part = TOK // 2
    x_cp = [[remote(own[m].at[pl.ds(k * part, part)], tokbuf.at[m, XP, pl.ds(k * part, part)], tx_s.at[m, k], tx_r.at[m, k], x_peer) for k in range(2)] for m in range(2)]
    d_cp = [[remote(tokbuf.at[m, XP, pl.ds(k * part, part)], tokbuf.at[m, DG, pl.ds(k * part, part)], td_s.at[m, k], td_r.at[m, k], core_peer) for k in range(2)] for m in range(2)]
    c_cp = [remote(own[m], tokbuf.at[m, CP], tc_s.at[m], tc_r.at[m], core_peer) for m in range(2)]
    for cp in (*xmeta_cp[0], *xmeta_cp[1], *cmeta_cp[0], *cmeta_cp[1], *x_cp[0], *c_cp):
        cp.start()
    local13 = (pltpu.make_async_copy(sw1, w13.at[SLOTS13 - 1, 0], w13_s.at[SLOTS13 - 1, 0]),
               pltpu.make_async_copy(sw3, w13.at[SLOTS13 - 1, 1], w13_s.at[SLOTS13 - 1, 1]))
    for cp in local13:
        cp.start()
    for u in range(SLOTS13 - 1):
        for cp in w13_copies(jnp.int32(u)):
            cp.start()

    half_d, half_f = D // 2, F // 2
    rows_d = pl.ds(pl.multiple_of(core * half_d, 128), half_d)
    rows_f = pl.ds(pl.multiple_of(core * half_f, 64), half_f)
    yw_cp = [remote(w.at[r], p.at[r], yw_s.at[i], yw_r.at[i], y_peer)
             for i, (w, p, r) in enumerate(((sw1, pw1, rows_d), (sw3, pw3, rows_d), (sw2, pw2, rows_f)))]
    fw_cp = [remote(p.at[r], p.at[r], fw_s.at[i], fw_r.at[i], core_peer)
             for i, (p, r) in enumerate(((pw1, rows_d), (pw3, rows_d), (pw2, rows_f)))]
    for cp in yw_cp:
        cp.start()
    for unit in range(SLOTS2):
        w2_copy(unit).start()

    for cp in own_cp:
        cp.wait()

    def route(i, carry):
        m, src = carry, i
        first = ep * EXP + lax.broadcasted_iota(jnp.int32, (EXP, TOK), 0)
        id_rows, slot_rows, gate_rows = ids[src, m, 0], ids[src, m, 1], gates[src, m]
        slot = jnp.full((EXP, TOK), -1, jnp.int32)
        gate = jnp.zeros((EXP, TOK), F32)
        for j in range(TOP_K):
            hit = (id_rows[j:j + 1, :] == first) & (slot_rows[j:j + 1, :] >= 0)
            slot = jnp.where(hit, slot_rows[j:j + 1, :], slot)
            gate = jnp.where(hit, gate_rows[j:j + 1, :], gate)
        pos = lax.broadcasted_iota(jnp.int32, (CAP, TOK), 0)
        for e in range(EXP):
            slots[m, src, e] = slot[e:e + 1, :]
        part = EXP // 2
        for k in range(2):
            g = jnp.concatenate([jnp.where(pos == slot[e:e + 1, :], gate[e:e + 1, :], 0.0)
                                 for e in range(k * part, (k + 1) * part)], axis=0).T
            hi = g.astype(BF16)
            g = g - hi.astype(F32)
            mid = g.astype(BF16)
            low = (g - mid.astype(F32)).astype(BF16)
            for p, v in enumerate((hi, mid, low)):
                gmat[m, src, :, pl.ds(p * EXP * CAP + k * part * CAP, part * CAP)] = v
        return carry

    def route_all(m):
        for cp in (*xmeta_cp[m], *cmeta_cp[m]):
            cp.wait()
        for cp in dmeta_cp[m]:
            cp.start()
        for cp in dmeta_cp[m]:
            cp.wait()
        lax.fori_loop(0, NSRC, route, jnp.int32(m))

    def arrive(m):
        c_cp[m].wait()
        for k in range(2):
            x_cp[m][k].wait()
            d_cp[m][k].start()

    def swiglu_in(x, w1, w3, store):
        full = F // COL
        for k in range(full):
            cols = pl.ds(k * COL, COL)
            a = dot(x, w1[:, cols])
            b = dot(x, w3[:, cols])
            store(cols, (jax.nn.silu(a) * b).astype(BF16))
        cols = pl.ds(full * COL, F - full * COL)
        ab = dot(x, jnp.concatenate([w1[:, cols], w3[:, cols]], axis=1))
        a, b = ab[:, :F - full * COL], ab[:, F - full * COL:]
        store(cols, (jax.nn.silu(a) * b).astype(BF16))

    def phase1(m, after_gather):
        def group(t, carry):
            g = lax.rem(t + m * (EXP // GRP - 1), EXP // GRP)
            pos = lax.broadcasted_iota(jnp.int32, (CAP, TOK), 0)
            for src in range(NSRC):
                place = jnp.concatenate([jnp.where(pos == slots[m, src, g * GRP + i], 1.0, 0.0) for i in range(GRP)], axis=0).astype(BF16)
                for n in range(NCOL):
                    cols = pl.ds(n * COL, COL)
                    r = dot(place, tokbuf[m, src, :, cols]).astype(BF16)
                    for i in range(GRP):
                        rowsg[i, pl.ds(src * CAP, CAP), cols] = r[i * CAP:(i + 1) * CAP]

            after_gather(t)

            def expert(i, carry):
                u = m * EXP + t * GRP + i
                slot = lax.rem(u, SLOTS13)
                rows = pl.ds(pl.multiple_of((g * GRP + i) * SIDE, SIDE), SIDE)
                near = pl.ds(pl.multiple_of((g * GRP + i) * ROWS + m * SIDE, SIDE), SIDE)

                @pl.when((u < EXP) | (u >= EXP + SLOTS13))
                def _():
                    for cp in w13_copies(u):
                        cp.wait()

                def store(cols, v):
                    hfar[rows, cols] = v[:SIDE]
                    hnear[near, cols] = v[SIDE:]

                swiglu_in(rowsg[i], w13.at[slot, 0], w13.at[slot, 1], store)
                nxt = u + SLOTS13

                @pl.when((nxt < EXP) | ((nxt >= EXP + SLOTS13) & (nxt < 2 * EXP)))
                def _():
                    for cp in w13_copies(nxt):
                        cp.start()
                return carry

            return lax.fori_loop(0, GRP, expert, carry)

        lax.fori_loop(0, EXP // GRP, group, 0)

    def expand(unit, first, h, sources):
        slot = lax.rem(unit, SLOTS2)
        size = sources * CAP
        for i in range(HALF):
            e = first + i
            y = dot(h[e * size:(e + 1) * size, :], w2b[slot, i]).astype(BF16)
            for k in range(sources):
                ybuf[k, e] = y[k * CAP:(k + 1) * CAP]

    def refill(unit):
        @pl.when(unit < 6 * NCOL)
        def _():
            w2_copy(unit).start()

    def combine(k, m, src):
        y = ybuf[k].reshape(EXP * CAP, COL)
        n = EXP * CAP
        g = gmat.at[m, src]
        return dot(g[:, :n], y) + dot(g[:, n:2 * n], y) + dot(g[:, 2 * n:], y)

    def far_copies(step):
        par = lax.rem(step, 2)
        return (remote(send.at[par], q2.at[step], p3_s.at[step], p3_r.at[step], core_peer),
                remote(q2.at[step], rr.at[step], rr_s.at[step], rr_r.at[step], x_peer))

    def near_copy(m, n):
        return remote(send.at[m], q0.at[m * NCOL + n], p1_s.at[m * NCOL + n], p1_r.at[m * NCOL + n], core_peer)

    def finish(step):
        cp, back = far_copies(step)
        cp.wait()
        q2[step] = q2[step] + tmp[lax.rem(step, 2)]
        back.start()

    def far(m):
        def column(n, carry):
            step = m * NCOL + n
            w2_copy(2 * step).wait()
            expand(2 * step, 0, hfar, 2)
            refill(2 * step + SLOTS2)
            w2_copy(2 * step + 1).wait()
            expand(2 * step + 1, HALF, hfar, 2)
            par = lax.rem(step, 2)
            send[par] = combine(DG, m, DG)
            tmp[par] = combine(XP, m, XP)
            far_copies(step)[0].start()
            refill(2 * step + 1 + SLOTS2)

            @pl.when(n >= 1)
            def _():
                finish(step - 1)
            return carry

        lax.fori_loop(0, NCOL, column, 0)

    def shared_in(half, slot):
        for m in range(2):
            def store(cols, v):
                hs_of(half, m)[:, cols] = v

            swiglu_in(tokbuf[m, OWN], w13.at[slot, 0], w13.at[slot, 1], store)

    def hs_of(half, m):
        rows = pl.ds(m * TOK, TOK)
        return hfar.at[rows, :] if half else hs.at[rows, :]

    route_all(0)
    route_all(1)
    for cp in local13:
        cp.wait()
    shared_in(0, SLOTS13 - 1)
    for cp in w13_copies(jnp.int32(SLOTS13 - 1)):
        cp.start()
    arrive(0)
    for cp in x_cp[1]:
        cp.start()
    for cp in d_cp[0]:
        cp.wait()
    phase1(0, lambda t: None)
    arrive(1)
    far(0)
    for cp in d_cp[1]:
        cp.wait()

    def between(t):
        @pl.when(t == 0)
        def _():
            finish(jnp.int32(NCOL - 1))

        @pl.when(t == 2)
        def _():
            for i in range(2):
                yw_cp[i].wait()
                fw_cp[i].start()

    phase1(1, between)

    peer13 = (pltpu.make_async_copy(pw1, w13.at[1, 0], w13_s.at[1, 0]), pltpu.make_async_copy(pw3, w13.at[1, 1], w13_s.at[1, 1]))

    def sw2_slot(half, n):
        return w13.at[2 + half, lax.div(n, 3), pl.ds(0, F), pl.ds(pl.multiple_of(lax.rem(n, 3) * COL, COL), COL)]

    def sw2_copy(half, n):
        return pltpu.make_async_copy((sw2, pw2)[half].at[:, pl.ds(pl.multiple_of(n * COL, COL), COL)], sw2_slot(half, n), sw2_s.at[n, half])

    for i in range(2):
        fw_cp[i].wait()
        peer13[i].start()
    far(1)
    for n in range(NCOL):
        sw2_copy(0, jnp.int32(n)).start()
    yw_cp[2].wait()
    fw_cp[2].start()
    finish(jnp.int32(2 * NCOL - 1))
    for cp in peer13:
        cp.wait()
    shared_in(1, 1)
    fw_cp[2].wait()
    for n in range(NCOL):
        sw2_copy(1, jnp.int32(n)).start()

    def near_finish(n):
        for m in range(2):
            near_copy(m, n).wait()
            q0[m * NCOL + n] = q0[m * NCOL + n] + tmp[m]

    def near_column(n, carry):
        step = 2 * NCOL + n
        w2_copy(2 * step).wait()
        expand(2 * step, 0, hnear, NSRC)
        refill(2 * step + SLOTS2)

        @pl.when(n >= 1)
        def _():
            near_finish(n - 1)

        w2_copy(2 * step + 1).wait()
        expand(2 * step + 1, HALF, hnear, NSRC)
        for m in range(2):
            send[m] = combine(2 * m + 1, m, CP)
        for m in range(2):
            tmp[m] = combine(2 * m, m, OWN)
        for m in range(2):
            near_copy(m, n).start()
        refill(2 * step + 1 + SLOTS2)
        for half in range(2):
            sw2_copy(half, n).wait()
        cols = pl.ds(pl.multiple_of(n * COL, COL), COL)
        for m in range(2):
            s = dot(hs_of(0, m)[...], sw2_slot(0, n)[...]) + dot(hs_of(1, m)[...], sw2_slot(1, n)[...])
            tmp[m] = tmp[m] + s + tokbuf[m, OWN, :, cols].astype(F32)
        return carry

    lax.fori_loop(0, NCOL, near_column, 0)
    near_finish(jnp.int32(NCOL - 1))

    out_cp = []
    for m, out in enumerate((oa, ob)):
        for n in range(NCOL):
            step = m * NCOL + n
            cols = pl.ds(n * COL, COL)
            far_copies(jnp.int32(step))[1].wait()
            tokbuf[m, XP, :, cols] = (q0[step] + rr[step]).astype(BF16)
            out_cp.append(pltpu.make_async_copy(tokbuf.at[m, XP, :, cols], out.at[:, cols], out_s.at[step]))
            out_cp[-1].start()
    for cp in out_cp:
        cp.wait()


def hand_over(a, b, oa, ob, buf, in_s, out_s):
    part = TOK // 4
    moves = [(src, dst, m, k) for m, (src, dst) in enumerate(((a, oa), (b, ob))) for k in range(4)]
    into = [pltpu.make_async_copy(src.at[pl.ds(k * part, part)], buf.at[m, pl.ds(k * part, part)], in_s.at[m, k]) for src, dst, m, k in moves]
    back = [pltpu.make_async_copy(buf.at[m, pl.ds(k * part, part)], dst.at[pl.ds(k * part, part)], out_s.at[m, k]) for src, dst, m, k in moves]
    for cp in into:
        cp.start()
    for i, o in zip(into, back):
        i.wait()
        o.start()
    for cp in back:
        cp.wait()


def solution(mesh):
    tok_spec = P(('data', 'ep', 'tp'), None)
    in_specs = (tok_spec,) * 8 + (P(None, 'tp'), P(None, 'tp'), P('tp', None), P('ep', None, None), P('ep', None, None), P('ep', None, None))

    def layer_local(tokens_a, tokens_b, experts_a, experts_b, gates_a, gates_b, slots_a, slots_b,
                    shared_w1, shared_w3, shared_w2, routed_w1, routed_w3, routed_w2):
        hbm = pl.BlockSpec(memory_space=pltpu.HBM)
        sem = pltpu.SemaphoreType.DMA
        steps = 2 * NCOL
        tok = jax.ShapeDtypeStruct((TOK, D), BF16)
        out = pl.pallas_call(
            kernel,
            name="moe_layer",
            out_shape=(tok, tok, jax.ShapeDtypeStruct((D, F), BF16), jax.ShapeDtypeStruct((D, F), BF16), jax.ShapeDtypeStruct((F, D), BF16)),
            in_specs=[hbm] * 14,
            out_specs=(hbm,) * 5,
            scratch_shapes=[
                pltpu.VMEM((NSRC, 2, 2, TOP_K, TOK), jnp.int32),
                pltpu.VMEM((NSRC, 2, TOP_K, TOK), F32),
                pltpu.VMEM((2, NSRC, TOK, D), BF16),
                pltpu.VMEM((2, NSRC, EXP, 1, TOK), jnp.int32),
                pltpu.VMEM((2, NSRC, TOK, 3 * EXP * CAP), BF16),
                pltpu.VMEM((GRP, ROWS, D), BF16),
                pltpu.VMEM((2 * TOK, F), BF16),
                pltpu.VMEM((EXP * SIDE, F), BF16),
                pltpu.VMEM((EXP * ROWS, F), BF16),
                pltpu.VMEM((NSRC, EXP, CAP, COL), BF16),
                pltpu.VMEM((2, TOK, COL), F32),
                pltpu.VMEM((2, TOK, COL), F32),
                pltpu.VMEM((steps, TOK, COL), F32),
                pltpu.VMEM((steps, TOK, COL), F32),
                pltpu.VMEM((steps, TOK, COL), F32),
                pltpu.VMEM((SLOTS13, 2, D, F), BF16),
                pltpu.VMEM((SLOTS2, HALF, F, COL), BF16),
                sem((2, 4)), sem((2, 2, 3)), sem((2, 2, 3)), sem((2, 3)), sem((2, 3)), sem((2,)), sem((2,)), sem((2, 2)), sem((2, 2)), sem((2, 2)), sem((2, 2)),
                sem((steps,)), sem((steps,)), sem((steps,)), sem((steps,)), sem((steps,)), sem((steps,)),
                sem((3,)), sem((3,)), sem((3,)), sem((3,)), sem((SLOTS13, 2)), sem((SLOTS2,)), sem((NCOL, 2)), sem((steps,)),
            ],
            compiler_params=pltpu.CompilerParams(collective_id=0, has_side_effects=True, vmem_limit_bytes=67043328),
        )(tokens_a, tokens_b, experts_a.T, experts_b.T, gates_a.T, gates_b.T, slots_a.T, slots_b.T,
          shared_w1, shared_w3, shared_w2, routed_w1, routed_w3, routed_w2)
        return tuple(pl.pallas_call(
            hand_over,
            name="hand_over",
            out_shape=(tok, tok),
            in_specs=[hbm] * 2,
            out_specs=(hbm,) * 2,
            scratch_shapes=[pltpu.VMEM((2, TOK, D), BF16), sem((2, 4)), sem((2, 4))],
        )(out[0], out[1]))

    return jax.shard_map(layer_local, mesh=mesh, in_specs=in_specs, out_specs=(tok_spec, tok_spec), check_vma=False)
```

time: 136 us -> 116 us (0.85)
  Pallas kernels: 129 us -> 115 us
  local copies, waits for them, and re-layouts: 3.93 us -> 0 us
  other arithmetic: 2.79 us -> 0 us
    pallas_call x1 -> x2, Pallas kernels: 129 us -> 115 us  [the longest x1 113 us: layer_local(): pl.pallas_call(kernel, name='moe_layer', out_shape=(tok, tok, jax.ShapeDt...]
    unnamed x2 -> x0, local copies, waits for them, and re-layouts: 3.93 us -> none
    transpose x2 -> x0, other arithmetic: 1.45 us -> none  [info(): return jnp.concatenate([row.T, gates.T], axis=0)]
where the time goes in v2:
time: 116 us
  Pallas kernels  115 us (99%)
    pallas_call x1, Pallas kernels, layer_local(): pl.pallas_call(kernel, name='moe_layer', out_shape=(tok, tok, jax.ShapeDt...  113 us

profile of v2, /device:TPU:0, one launch (start us, length us, event | category | flops | bytes accessed | tf_op | source)
XLA Modules:
  0.0 115.6 jit_solution(6394353739493489540)
XLA Ops:
  0.6 112.6 %moe_layer.1 = (bf16[256,1280]{1,0:T(8,128)(2,1)}, bf16[256,1280]{1,0:T(8,128)(2,1)}, bf16[1280,896]{1,0:T(8,128)(2,1)}, bf16[1280,896]{1,0:T(8,128)(2,1)}, bf16[896,1280]{1,0:T(8,128)(2,1)}) custom-call(bf16[256,1280]{1,0:T(8,128)(2,1)} %xa.1, bf16[256,1280]{1,0:T(8,128)(2,1)} %xb.1, s32[6,256]{1,0:T(8,128)} %bitcast.6, s32[6,256]{1,0:T(8,128)} %bitcast.7, ...), custom_call_target="tpu_custom_call" | custom-call | tf_op jit(solution)/shard_map/moe_layer/pallas_call | solution.py:405
  113.3 2.2 %hand_over.1 = (bf16[256,1280]{1,0:T(8,128)(2,1)}, bf16[256,1280]{1,0:T(8,128)(2,1)}) custom-call(bf16[256,1280]{1,0:T(8,128)(2,1)} %get-tuple-element.4.a, bf16[256,1280]{1,0:T(8,128)(2,1)} %get-tuple-element.5.b), custom_call_target="tpu_custom_call" | custom-call | tf_op jit(solution)/shard_map/hand_over/pallas_call | solution.py:436

commit v3 on v2

--- a/solution.py
+++ b/solution.py
@@ -25,8 +25,9 @@
 ROWS = NSRC * CAP
 SIDE = 2 * CAP
 SLOTS13 = 4
-SLOTS2 = 3
-HALF = EXP // 2
+SLOTS2 = 5
+PER = 4
+BLOCKS = EXP // PER
 
 
 def dot(a, b):
@@ -35,9 +36,9 @@
 
 def kernel(xa, xb, ea, eb, ga, gb, sa, sb, sw1, sw3, sw2, rw1, rw3, rw2,
            oa, ob, pw1, pw3, pw2,
-           ids, gates, tokbuf, slots, gmat, rowsg, hs, hfar, hnear, ybuf, send, tmp, q0, q2, rr, w13, w2b,
+           ids, gates, tokbuf, slots, gmat, rowsg, hs, hfar, hnear, ybuf, work, q0, q2, rr, w13, w2b,
            own_s, meta_s, meta_r, fmeta_s, fmeta_r, tc_s, tc_r, tx_s, tx_r, td_s, td_r, p1_s, p1_r, p3_s, p3_r, rr_s, rr_r,
-           yw_s, yw_r, fw_s, fw_r, w13_s, w2_s, sw2_s, out_s):
+           yw_s, yw_r, fw_s, fw_r, w13_s, w2_s, sw2_s):
     ep = lax.axis_index("ep")
     tp = lax.axis_index("tp")
     core = lax.rem(ep, 2)
@@ -61,9 +62,9 @@
 
     def w2_copy(unit):
         slot = lax.rem(unit, SLOTS2)
-        n = lax.rem(lax.div(unit, 2), NCOL)
-        first = lax.rem(unit, 2) * HALF
-        return pltpu.make_async_copy(rw2.at[pl.ds(first, HALF), :, pl.ds(pl.multiple_of(n * COL, COL), COL)], w2b.at[slot], w2_s.at[slot])
+        n = lax.rem(lax.div(unit, BLOCKS), NCOL)
+        first = lax.rem(unit, BLOCKS) * PER
+        return pltpu.make_async_copy(rw2.at[pl.ds(first, PER), :, pl.ds(pl.multiple_of(n * COL, COL), COL)], w2b.at[slot], w2_s.at[slot])
 
     routing = ((ea, sa, ga), (eb, sb, gb))
 
@@ -110,7 +111,7 @@
     for cp in yw_cp:
         cp.start()
     for unit in range(SLOTS2):
-        w2_copy(unit).start()
+        w2_copy(jnp.int32(unit)).start()
 
     for cp in own_cp:
         cp.wait()
@@ -150,7 +151,6 @@
         lax.fori_loop(0, NSRC, route, jnp.int32(m))
 
     def arrive(m):
-        c_cp[m].wait()
         for k in range(2):
             x_cp[m][k].wait()
             d_cp[m][k].start()
@@ -167,18 +167,35 @@
         a, b = ab[:, :F - full * COL], ab[:, F - full * COL:]
         store(cols, (jax.nn.silu(a) * b).astype(BF16))
 
+    def gather(g, places):
+        pos = lax.broadcasted_iota(jnp.int32, (CAP, TOK), 0)
+        for k, (m, src) in enumerate(places):
+            place = jnp.concatenate([jnp.where(pos == slots[m, src, g * GRP + i], 1.0, 0.0) for i in range(GRP)], axis=0).astype(BF16)
+            for n in range(NCOL):
+                cols = pl.ds(n * COL, COL)
+                r = dot(place, tokbuf[m, src, :, cols]).astype(BF16)
+                for i in range(GRP):
+                    rowsg[i, pl.ds(k * CAP, CAP), cols] = r[i * CAP:(i + 1) * CAP]
+
+    def early():
+        gather(0, [(m, src) for m in range(2) for src in (OWN, CP)])
+
+        def expert(i, carry):
+            for cp in w13_copies(i):
+                cp.wait()
+            rows = pl.ds(pl.multiple_of(i * ROWS, ROWS), ROWS)
+
+            def store(cols, v):
+                hnear[rows, cols] = v
+
+            swiglu_in(rowsg[i], w13.at[i, 0], w13.at[i, 1], store)
+            return carry
+
+        lax.fori_loop(0, GRP, expert, 0)
+
     def phase1(m, after_gather):
-        def group(t, carry):
-            g = lax.rem(t + m * (EXP // GRP - 1), EXP // GRP)
-            pos = lax.broadcasted_iota(jnp.int32, (CAP, TOK), 0)
-            for src in range(NSRC):
-                place = jnp.concatenate([jnp.where(pos == slots[m, src, g * GRP + i], 1.0, 0.0) for i in range(GRP)], axis=0).astype(BF16)
-                for n in range(NCOL):
-                    cols = pl.ds(n * COL, COL)
-                    r = dot(place, tokbuf[m, src, :, cols]).astype(BF16)
-                    for i in range(GRP):
-                        rowsg[i, pl.ds(src * CAP, CAP), cols] = r[i * CAP:(i + 1) * CAP]
-
+        def run(t, g, all_rows):
+            gather(g, [(m, src) for src in ((XP, DG, OWN, CP) if all_rows else (XP, DG))])
             after_gather(t)
 
             def expert(i, carry):
@@ -187,16 +204,17 @@
                 rows = pl.ds(pl.multiple_of((g * GRP + i) * SIDE, SIDE), SIDE)
                 near = pl.ds(pl.multiple_of((g * GRP + i) * ROWS + m * SIDE, SIDE), SIDE)
 
-                @pl.when((u < EXP) | (u >= EXP + SLOTS13))
+                @pl.when((u >= SLOTS13) & ((u < EXP) | (u >= EXP + SLOTS13)))
                 def _():
                     for cp in w13_copies(u):
                         cp.wait()
 
                 def store(cols, v):
                     hfar[rows, cols] = v[:SIDE]
-                    hnear[near, cols] = v[SIDE:]
-
-                swiglu_in(rowsg[i], w13.at[slot, 0], w13.at[slot, 1], store)
+                    if all_rows:
+                        hnear[near, cols] = v[SIDE:]
+
+                swiglu_in(rowsg[i] if all_rows else rowsg[i, :SIDE], w13.at[slot, 0], w13.at[slot, 1], store)
                 nxt = u + SLOTS13
 
                 @pl.when((nxt < EXP) | ((nxt >= EXP + SLOTS13) & (nxt < 2 * EXP)))
@@ -205,23 +223,35 @@
                         cp.start()
                 return carry
 
-            return lax.fori_loop(0, GRP, expert, carry)
+            lax.fori_loop(0, GRP, expert, 0)
+
+        def group(t, carry):
+            g = lax.rem(t + m * (EXP // GRP - 1), EXP // GRP)
+
+            @pl.when(g == 0)
+            def _():
+                run(t, g, False)
+
+            @pl.when(g > 0)
+            def _():
+                run(t, g, True)
+            return carry
 
         lax.fori_loop(0, EXP // GRP, group, 0)
 
-    def expand(unit, first, h, sources):
-        slot = lax.rem(unit, SLOTS2)
+    def expand(step, h, sources, blocks=range(BLOCKS), refills=BLOCKS):
         size = sources * CAP
-        for i in range(HALF):
-            e = first + i
-            y = dot(h[e * size:(e + 1) * size, :], w2b[slot, i]).astype(BF16)
-            for k in range(sources):
-                ybuf[k, e] = y[k * CAP:(k + 1) * CAP]
-
-    def refill(unit):
-        @pl.when(unit < 6 * NCOL)
-        def _():
-            w2_copy(unit).start()
+        for b in blocks:
+            w2_copy(step * BLOCKS + b).wait()
+        for b in blocks:
+            slot = lax.rem(step * BLOCKS + b, SLOTS2)
+            for i in range(PER):
+                e = b * PER + i
+                y = dot(h[e * size:(e + 1) * size, :], w2b[slot, i]).astype(BF16)
+                for k in range(sources):
+                    ybuf[k, e] = y[k * CAP:(k + 1) * CAP]
+            if b < refills:
+                w2_copy(step * BLOCKS + b + SLOTS2).start()
 
     def combine(k, m, src):
         y = ybuf[k].reshape(EXP * CAP, COL)
@@ -231,33 +261,36 @@
 
     def far_copies(step):
         par = lax.rem(step, 2)
-        return (remote(send.at[par], q2.at[step], p3_s.at[step], p3_r.at[step], core_peer),
+        return (remote(work.at[par], q2.at[step], p3_s.at[step], p3_r.at[step], core_peer),
                 remote(q2.at[step], rr.at[step], rr_s.at[step], rr_r.at[step], x_peer))
 
     def near_copy(m, n):
-        return remote(send.at[m], q0.at[m * NCOL + n], p1_s.at[m * NCOL + n], p1_r.at[m * NCOL + n], core_peer)
+        return remote(work.at[2 * lax.rem(n, 2) + m], q0.at[m * NCOL + n], p1_s.at[m * NCOL + n], p1_r.at[m * NCOL + n], core_peer)
 
     def finish(step):
         cp, back = far_copies(step)
         cp.wait()
-        q2[step] = q2[step] + tmp[lax.rem(step, 2)]
+        q2[step] = q2[step] + work[2 + lax.rem(step, 2)]
         back.start()
 
-    def far(m):
+    def far(m, during):
         def column(n, carry):
             step = m * NCOL + n
-            w2_copy(2 * step).wait()
-            expand(2 * step, 0, hfar, 2)
-            refill(2 * step + SLOTS2)
-            w2_copy(2 * step + 1).wait()
-            expand(2 * step + 1, HALF, hfar, 2)
+            expand(step, hfar, 2, range(BLOCKS // 2))
+
+            @pl.when(n == 1)
+            def _():
+                finish(step - 1)
+
+            expand(step, hfar, 2, range(BLOCKS // 2, BLOCKS))
             par = lax.rem(step, 2)
-            send[par] = combine(DG, m, DG)
-            tmp[par] = combine(XP, m, XP)
+            work[par] = combine(DG, m, DG)
+            work[2 + par] = combine(XP, m, XP)
             far_copies(step)[0].start()
-            refill(2 * step + 1 + SLOTS2)
-
-            @pl.when(n >= 1)
+
+            during(n)
+
+            @pl.when(n >= 2)
             def _():
                 finish(step - 1)
             return carry
@@ -275,13 +308,16 @@
         rows = pl.ds(m * TOK, TOK)
         return hfar.at[rows, :] if half else hs.at[rows, :]
 
+    for cp in local13:
+        cp.wait()
+    shared_in(0, SLOTS13 - 1)
+    for cp in w13_copies(jnp.int32(SLOTS13 - 1)):
+        cp.start()
     route_all(0)
     route_all(1)
-    for cp in local13:
-        cp.wait()
-    shared_in(0, SLOTS13 - 1)
-    for cp in w13_copies(jnp.int32(SLOTS13 - 1)):
-        cp.start()
+    for cp in c_cp:
+        cp.wait()
+    early()
     arrive(0)
     for cp in x_cp[1]:
         cp.start()
@@ -289,12 +325,12 @@
         cp.wait()
     phase1(0, lambda t: None)
     arrive(1)
-    far(0)
+    far(0, lambda n: None)
     for cp in d_cp[1]:
         cp.wait()
 
     def between(t):
-        @pl.when(t == 0)
+        @pl.when(t == 1)
         def _():
             finish(jnp.int32(NCOL - 1))
 
@@ -314,82 +350,73 @@
     def sw2_copy(half, n):
         return pltpu.make_async_copy((sw2, pw2)[half].at[:, pl.ds(pl.multiple_of(n * COL, COL), COL)], sw2_slot(half, n), sw2_s.at[n, half])
 
-    for i in range(2):
-        fw_cp[i].wait()
-        peer13[i].start()
-    far(1)
+
+    def fetch_peer(n):
+        for i in range(2):
+            @pl.when(n == 2 + i)
+            def _():
+                fw_cp[i].wait()
+                peer13[i].start()
+
+        @pl.when(n == 3)
+        def _():
+            yw_cp[2].wait()
+            fw_cp[2].start()
+
+    far(1, fetch_peer)
     for n in range(NCOL):
         sw2_copy(0, jnp.int32(n)).start()
-    yw_cp[2].wait()
-    fw_cp[2].start()
-    finish(jnp.int32(2 * NCOL - 1))
-    for cp in peer13:
-        cp.wait()
-    shared_in(1, 1)
     fw_cp[2].wait()
     for n in range(NCOL):
         sw2_copy(1, jnp.int32(n)).start()
+    for cp in peer13:
+        cp.wait()
+    shared_in(1, 1)
+    finish(jnp.int32(2 * NCOL - 1))
 
     def near_finish(n):
         for m in range(2):
+            step = m * NCOL + n
             near_copy(m, n).wait()
-            q0[m * NCOL + n] = q0[m * NCOL + n] + tmp[m]
-
-    def near_column(n, carry):
-        step = 2 * NCOL + n
-        w2_copy(2 * step).wait()
-        expand(2 * step, 0, hnear, NSRC)
-        refill(2 * step + SLOTS2)
+            back = far_copies(step)[1]
+            back.wait_recv()
+            if m:
+                back.wait_send()
+            mine = q2[2 * lax.rem(n, 2) + m]
+            (oa, ob)[m][:, pl.ds(pl.multiple_of(n * COL, COL), COL)] = (q0[step] + rr[step] + mine).astype(BF16)
+
+    for n in range(NCOL):
+        far_copies(jnp.int32(n))[1].wait_send()
+
+    def near_column(n, carry, refills=BLOCKS, final=False):
+        for half in range(2):
+            sw2_copy(half, n).wait()
+        expand(2 * NCOL + n, hnear, NSRC, refills=refills)
+        base = 2 * lax.rem(n, 2)
+        cols = pl.ds(pl.multiple_of(n * COL, COL), COL)
+        for m in range(2):
+            work[base + m] = combine(2 * m + 1, m, CP)
+        if final:
+            for m in range(2):
+                near_copy(m, n).start()
+        for m in range(2):
+            s = dot(hs_of(0, m)[...], sw2_slot(0, n)[...]) + dot(hs_of(1, m)[...], sw2_slot(1, n)[...])
+            q2[base + m] = s + tokbuf[m, OWN, :, cols].astype(F32) + combine(2 * m, m, OWN)
+        if not final:
+            for m in range(2):
+                near_copy(m, n).start()
 
         @pl.when(n >= 1)
         def _():
             near_finish(n - 1)
-
-        w2_copy(2 * step + 1).wait()
-        expand(2 * step + 1, HALF, hnear, NSRC)
-        for m in range(2):
-            send[m] = combine(2 * m + 1, m, CP)
-        for m in range(2):
-            tmp[m] = combine(2 * m, m, OWN)
-        for m in range(2):
-            near_copy(m, n).start()
-        refill(2 * step + 1 + SLOTS2)
-        for half in range(2):
-            sw2_copy(half, n).wait()
-        cols = pl.ds(pl.multiple_of(n * COL, COL), COL)
-        for m in range(2):
-            s = dot(hs_of(0, m)[...], sw2_slot(0, n)[...]) + dot(hs_of(1, m)[...], sw2_slot(1, n)[...])
-            tmp[m] = tmp[m] + s + tokbuf[m, OWN, :, cols].astype(F32)
         return carry
 
-    lax.fori_loop(0, NCOL, near_column, 0)
+    last = NCOL * BLOCKS * 3 - SLOTS2
+    full = (last - 2 * NCOL * BLOCKS) // BLOCKS
+    lax.fori_loop(0, full, near_column, 0)
+    for n in range(full, NCOL):
+        near_column(jnp.int32(n), 0, max(0, last - (2 * NCOL + n) * BLOCKS), n == NCOL - 1)
     near_finish(jnp.int32(NCOL - 1))
-
-    out_cp = []
-    for m, out in enumerate((oa, ob)):
-        for n in range(NCOL):
-            step = m * NCOL + n
-            cols = pl.ds(n * COL, COL)
-            far_copies(jnp.int32(step))[1].wait()
-            tokbuf[m, XP, :, cols] = (q0[step] + rr[step]).astype(BF16)
-            out_cp.append(pltpu.make_async_copy(tokbuf.at[m, XP, :, cols], out.at[:, cols], out_s.at[step]))
-            out_cp[-1].start()
-    for cp in out_cp:
-        cp.wait()
-
-
-def hand_over(a, b, oa, ob, buf, in_s, out_s):
-    part = TOK // 4
-    moves = [(src, dst, m, k) for m, (src, dst) in enumerate(((a, oa), (b, ob))) for k in range(4)]
-    into = [pltpu.make_async_copy(src.at[pl.ds(k * part, part)], buf.at[m, pl.ds(k * part, part)], in_s.at[m, k]) for src, dst, m, k in moves]
-    back = [pltpu.make_async_copy(buf.at[m, pl.ds(k * part, part)], dst.at[pl.ds(k * part, part)], out_s.at[m, k]) for src, dst, m, k in moves]
-    for cp in into:
-        cp.start()
-    for i, o in zip(into, back):
-        i.wait()
-        o.start()
-    for cp in back:
-        cp.wait()
 
 
 def solution(mesh):
@@ -399,15 +426,16 @@
     def layer_local(tokens_a, tokens_b, experts_a, experts_b, gates_a, gates_b, slots_a, slots_b,
                     shared_w1, shared_w3, shared_w2, routed_w1, routed_w3, routed_w2):
         hbm = pl.BlockSpec(memory_space=pltpu.HBM)
+        vmem = pl.BlockSpec(memory_space=pltpu.VMEM)
         sem = pltpu.SemaphoreType.DMA
         steps = 2 * NCOL
         tok = jax.ShapeDtypeStruct((TOK, D), BF16)
         out = pl.pallas_call(
             kernel,
             name="moe_layer",
-            out_shape=(tok, tok, jax.ShapeDtypeStruct((D, F), BF16), jax.ShapeDtypeStruct((D, F), BF16), jax.ShapeDtypeStruct((F, D), BF16)),
+            out_shape=(pltpu.VMEM((TOK, D), BF16), pltpu.VMEM((TOK, D), BF16), jax.ShapeDtypeStruct((D, F), BF16), jax.ShapeDtypeStruct((D, F), BF16), jax.ShapeDtypeStruct((F, D), BF16)),
             in_specs=[hbm] * 14,
-            out_specs=(hbm,) * 5,
+            out_specs=(vmem,) * 2 + (hbm,) * 3,
             scratch_shapes=[
                 pltpu.VMEM((NSRC, 2, 2, TOP_K, TOK), jnp.int32),
                 pltpu.VMEM((NSRC, 2, TOP_K, TOK), F32),
@@ -419,27 +447,19 @@
                 pltpu.VMEM((EXP * SIDE, F), BF16),
                 pltpu.VMEM((EXP * ROWS, F), BF16),
                 pltpu.VMEM((NSRC, EXP, CAP, COL), BF16),
-                pltpu.VMEM((2, TOK, COL), F32),
-                pltpu.VMEM((2, TOK, COL), F32),
+                pltpu.VMEM((4, TOK, COL), F32),
                 pltpu.VMEM((steps, TOK, COL), F32),
                 pltpu.VMEM((steps, TOK, COL), F32),
                 pltpu.VMEM((steps, TOK, COL), F32),
                 pltpu.VMEM((SLOTS13, 2, D, F), BF16),
-                pltpu.VMEM((SLOTS2, HALF, F, COL), BF16),
+                pltpu.VMEM((SLOTS2, PER, F, COL), BF16),
                 sem((2, 4)), sem((2, 2, 3)), sem((2, 2, 3)), sem((2, 3)), sem((2, 3)), sem((2,)), sem((2,)), sem((2, 2)), sem((2, 2)), sem((2, 2)), sem((2, 2)),
                 sem((steps,)), sem((steps,)), sem((steps,)), sem((steps,)), sem((steps,)), sem((steps,)),
-                sem((3,)), sem((3,)), sem((3,)), sem((3,)), sem((SLOTS13, 2)), sem((SLOTS2,)), sem((NCOL, 2)), sem((steps,)),
+                sem((3,)), sem((3,)), sem((3,)), sem((3,)), sem((SLOTS13, 2)), sem((SLOTS2,)), sem((NCOL, 2)),
             ],
-            compiler_params=pltpu.CompilerParams(collective_id=0, has_side_effects=True, vmem_limit_bytes=67043328),
+            compiler_params=pltpu.CompilerParams(collective_id=0, has_side_effects=True, vmem_limit_bytes=67043328 - 1376256),
         )(tokens_a, tokens_b, experts_a.T, experts_b.T, gates_a.T, gates_b.T, slots_a.T, slots_b.T,
           shared_w1, shared_w3, shared_w2, routed_w1, routed_w3, routed_w2)
-        return tuple(pl.pallas_call(
-            hand_over,
-            name="hand_over",
-            out_shape=(tok, tok),
-            in_specs=[hbm] * 2,
-            out_specs=(hbm,) * 2,
-            scratch_shapes=[pltpu.VMEM((2, TOK, D), BF16), sem((2, 4)), sem((2, 4))],
-        )(out[0], out[1]))
+        return out[0], out[1]
 
     return jax.shard_map(layer_local, mesh=mesh, in_specs=in_specs, out_specs=(tok_spec, tok_spec), check_vma=False)

time: 116 us -> 110 us (0.948)
  Pallas kernels: 115 us -> 108 us
  local copies, waits for them, and re-layouts: 0 us -> 1.67 us
    pallas_call x2 -> x1, Pallas kernels: 115 us -> 108 us  [layer_local(): pl.pallas_call(kernel, name='moe_layer', out_shape=(pltpu.VMEM((TOK, D),...]
    unnamed x0 -> x2, local copies, waits for them, and re-layouts: none -> 1.67 us
where the time goes in v3:
time: 110 us
  Pallas kernels  108 us (98%)
  local copies, waits for them, and re-layouts  1.67 us (2%)
    pallas_call x1, Pallas kernels, layer_local(): pl.pallas_call(kernel, name='moe_layer', out_shape=(pltpu.VMEM((TOK, D),...  108 us

profile of v3, /device:TPU:0, one launch (start us, length us, event | category | flops | bytes accessed | tf_op | source)
XLA Modules:
  0.0 109.9 jit_solution(13770855863591374487)
XLA Ops:
  0.6 107.6 %moe_layer.1 = (bf16[256,1280]{1,0:T(8,128)(2,1)S(1)}, bf16[256,1280]{1,0:T(8,128)(2,1)S(1)}, bf16[1280,896]{1,0:T(8,128)(2,1)}, bf16[1280,896]{1,0:T(8,128)(2,1)}, bf16[896,1280]{1,0:T(8,128)(2,1)}) custom-call(bf16[256,1280]{1,0:T(8,128)(2,1)} %xa.1, bf16[256,1280]{1,0:T(8,128)(2,1)} %xb.1, s32[6,256]{1,0:T(8,128)} %bitcast.6, s32[6,256]{1,0:T(8,128)} %bitcast.7, ...), custom_call_target="tpu_custom_call" | custom-call | tf_op jit(solution)/shard_map/moe_layer/pallas_call | solution.py:433
  108.3 0.8 copy.18
  109.1 0.8 copy.19

commit v4 on v3

--- a/solution.py
+++ b/solution.py
@@ -261,11 +261,11 @@
 
     def far_copies(step):
         par = lax.rem(step, 2)
-        return (remote(work.at[par], q2.at[step], p3_s.at[step], p3_r.at[step], core_peer),
+        return (remote(work.at[par], q2.at[step], p3_s.at[par], p3_r.at[step], core_peer),
                 remote(q2.at[step], rr.at[step], rr_s.at[step], rr_r.at[step], x_peer))
 
     def near_copy(m, n):
-        return remote(work.at[2 * lax.rem(n, 2) + m], q0.at[m * NCOL + n], p1_s.at[m * NCOL + n], p1_r.at[m * NCOL + n], core_peer)
+        return remote(work.at[2 * lax.rem(n, 2) + m], q0.at[m * NCOL + n], p1_s.at[2 * lax.rem(n, 2) + m], p1_r.at[m * NCOL + n], core_peer)
 
     def finish(step):
         cp, back = far_copies(step)
@@ -278,9 +278,10 @@
             step = m * NCOL + n
             expand(step, hfar, 2, range(BLOCKS // 2))
 
-            @pl.when(n == 1)
-            def _():
-                finish(step - 1)
+            if m:
+                @pl.when(n == 1)
+                def _():
+                    finish(step - 1)
 
             expand(step, hfar, 2, range(BLOCKS // 2, BLOCKS))
             par = lax.rem(step, 2)
@@ -290,7 +291,7 @@
 
             during(n)
 
-            @pl.when(n >= 2)
+            @pl.when(n >= 1 + m)
             def _():
                 finish(step - 1)
             return carry
@@ -400,7 +401,8 @@
             for m in range(2):
                 near_copy(m, n).start()
         for m in range(2):
-            s = dot(hs_of(0, m)[...], sw2_slot(0, n)[...]) + dot(hs_of(1, m)[...], sw2_slot(1, n)[...])
+            s = dot(jnp.concatenate([hs_of(half, m)[...] for half in range(2)], axis=1),
+                    jnp.concatenate([sw2_slot(half, n)[...] for half in range(2)], axis=0))
             q2[base + m] = s + tokbuf[m, OWN, :, cols].astype(F32) + combine(2 * m, m, OWN)
         if not final:
             for m in range(2):
@@ -417,6 +419,14 @@
     for n in range(full, NCOL):
         near_column(jnp.int32(n), 0, max(0, last - (2 * NCOL + n) * BLOCKS), n == NCOL - 1)
     near_finish(jnp.int32(NCOL - 1))
+
+
+def hand_over(a, b, oa, ob, out_s):
+    copies = [pltpu.make_async_copy(src, dst, out_s.at[m]) for m, (src, dst) in enumerate(((a, oa), (b, ob)))]
+    for cp in copies:
+        cp.start()
+    for cp in copies:
+        cp.wait()
 
 
 def solution(mesh):
@@ -454,12 +464,19 @@
                 pltpu.VMEM((SLOTS13, 2, D, F), BF16),
                 pltpu.VMEM((SLOTS2, PER, F, COL), BF16),
                 sem((2, 4)), sem((2, 2, 3)), sem((2, 2, 3)), sem((2, 3)), sem((2, 3)), sem((2,)), sem((2,)), sem((2, 2)), sem((2, 2)), sem((2, 2)), sem((2, 2)),
-                sem((steps,)), sem((steps,)), sem((steps,)), sem((steps,)), sem((steps,)), sem((steps,)),
+                sem((4,)), sem((steps,)), sem((2,)), sem((steps,)), sem((steps,)), sem((steps,)),
                 sem((3,)), sem((3,)), sem((3,)), sem((3,)), sem((SLOTS13, 2)), sem((SLOTS2,)), sem((NCOL, 2)),
             ],
             compiler_params=pltpu.CompilerParams(collective_id=0, has_side_effects=True, vmem_limit_bytes=67043328 - 1376256),
         )(tokens_a, tokens_b, experts_a.T, experts_b.T, gates_a.T, gates_b.T, slots_a.T, slots_b.T,
           shared_w1, shared_w3, shared_w2, routed_w1, routed_w3, routed_w2)
-        return out[0], out[1]
+        return tuple(pl.pallas_call(
+            hand_over,
+            name="hand_over",
+            out_shape=(tok, tok),
+            in_specs=[vmem] * 2,
+            out_specs=(hbm,) * 2,
+            scratch_shapes=[sem((2,))],
+        )(*[pltpu.with_memory_space_constraint(o, pltpu.VMEM) for o in out[:2]]))
 
     return jax.shard_map(layer_local, mesh=mesh, in_specs=in_specs, out_specs=(tok_spec, tok_spec), check_vma=False)

time: 110 us -> 109 us (level)
  local copies, waits for them, and re-layouts: 1.67 us -> 0 us
    unnamed x2 -> x0, local copies, waits for them, and re-layouts: 1.67 us -> none
where the time goes in v4:
time: 109 us
  Pallas kernels  108 us (99%)
    pallas_call x1, Pallas kernels, layer_local(): pl.pallas_call(kernel, name='moe_layer', out_shape=(pltpu.VMEM((TOK, D),...  107 us

profile of v4, /device:TPU:0, one launch (start us, length us, event | category | flops | bytes accessed | tf_op | source)
XLA Modules:
  0.0 108.8 jit_solution(10872802001504993532)
XLA Ops:
  0.6 106.9 %moe_layer.1 = (bf16[256,1280]{1,0:T(8,128)(2,1)S(1)}, bf16[256,1280]{1,0:T(8,128)(2,1)S(1)}, bf16[1280,896]{1,0:T(8,128)(2,1)}, bf16[1280,896]{1,0:T(8,128)(2,1)}, bf16[896,1280]{1,0:T(8,128)(2,1)}) custom-call(bf16[256,1280]{1,0:T(8,128)(2,1)} %xa.1, bf16[256,1280]{1,0:T(8,128)(2,1)} %xb.1, s32[6,256]{1,0:T(8,128)} %bitcast.6, s32[6,256]{1,0:T(8,128)} %bitcast.7, ...), custom_call_target="tpu_custom_call" | custom-call | tf_op jit(solution)/shard_map/moe_layer/pallas_call | solution.py:443
  107.5 1.1 hand_over.1

commit v5 on v4

--- a/solution.py
+++ b/solution.py
@@ -36,7 +36,7 @@
 
 def kernel(xa, xb, ea, eb, ga, gb, sa, sb, sw1, sw3, sw2, rw1, rw3, rw2,
            oa, ob, pw1, pw3, pw2,
-           ids, gates, tokbuf, slots, gmat, rowsg, hs, hfar, hnear, ybuf, work, q0, q2, rr, w13, w2b,
+           raw, ids, gates, tokbuf, slots, gmat, rowsg, hs, hfar, hnear, ybuf, work, q0, q2, rr, w13, w2b,
            own_s, meta_s, meta_r, fmeta_s, fmeta_r, tc_s, tc_r, tx_s, tx_r, td_s, td_r, p1_s, p1_r, p3_s, p3_r, rr_s, rr_r,
            yw_s, yw_r, fw_s, fw_r, w13_s, w2_s, sw2_s):
     ep = lax.axis_index("ep")
@@ -44,7 +44,6 @@
     core = lax.rem(ep, 2)
     core_peer = {"ep": ep + 1 - 2 * core}
     x_peer = {"ep": lax.rem(ep + 2, 4)}
-    diag = {"ep": 3 - ep}
     y_peer = {"tp": 1 - tp}
     own = (xa, xb)
 
@@ -69,28 +68,32 @@
     routing = ((ea, sa, ga), (eb, sb, gb))
 
     def routing_slots(m, src):
-        return ids.at[src, m, 0], ids.at[src, m, 1], gates.at[src, m]
+        return ids.at[src, m], gates.at[src, m]
 
     own_cp = [pltpu.make_async_copy(a, b, own_s.at[m, k]) for m in range(2)
-              for k, (a, b) in enumerate(zip((*routing[m], own[m]), (*routing_slots(m, OWN), tokbuf.at[m, OWN])))]
+              for k, (a, b) in enumerate(zip((*routing[m], own[m]), (raw.at[m, 0], raw.at[m, 1], gates.at[OWN, m], tokbuf.at[m, OWN])))]
     for cp in own_cp:
         cp.start()
 
     barrier = pltpu.get_barrier_semaphore()
-    for dev in (core_peer, x_peer, diag, y_peer):
+    for dev in (core_peer, x_peer, y_peer):
         pl.semaphore_signal(barrier, inc=1, device_id=dev, device_id_type=MESH)
-    pl.semaphore_wait(barrier, 4)
+    pl.semaphore_wait(barrier, 3)
+    for cp in own_cp:
+        cp.wait()
+    for m in range(2):
+        ids[OWN, m] = jnp.where(raw[m, 1] >= 0, raw[m, 0] * CAP + raw[m, 1], -1)
 
     def routing_cp(m, k, src, dst, ss, rs, dev):
         return remote(src[k], routing_slots(m, dst)[k], ss.at[m, k], rs.at[m, k], dev)
 
-    cmeta_cp = [[routing_cp(m, k, routing[m], CP, meta_s.at[0], meta_r.at[0], core_peer) for k in range(3)] for m in range(2)]
-    xmeta_cp = [[routing_cp(m, k, routing[m], XP, meta_s.at[1], meta_r.at[1], x_peer) for k in range(3)] for m in range(2)]
-    dmeta_cp = [[routing_cp(m, k, routing_slots(m, XP), DG, fmeta_s, fmeta_r, core_peer) for k in range(3)] for m in range(2)]
-    part = TOK // 2
-    x_cp = [[remote(own[m].at[pl.ds(k * part, part)], tokbuf.at[m, XP, pl.ds(k * part, part)], tx_s.at[m, k], tx_r.at[m, k], x_peer) for k in range(2)] for m in range(2)]
-    d_cp = [[remote(tokbuf.at[m, XP, pl.ds(k * part, part)], tokbuf.at[m, DG, pl.ds(k * part, part)], td_s.at[m, k], td_r.at[m, k], core_peer) for k in range(2)] for m in range(2)]
-    c_cp = [remote(own[m], tokbuf.at[m, CP], tc_s.at[m], tc_r.at[m], core_peer) for m in range(2)]
+    cmeta_cp = [[routing_cp(m, k, routing_slots(m, OWN), CP, meta_s.at[0], meta_r.at[0], core_peer) for k in range(2)] for m in range(2)]
+    xmeta_cp = [[routing_cp(m, k, routing_slots(m, OWN), XP, meta_s.at[1], meta_r.at[1], x_peer) for k in range(2)] for m in range(2)]
+    dmeta_cp = [[routing_cp(m, k, routing_slots(m, XP), DG, fmeta_s, fmeta_r, core_peer) for k in range(2)] for m in range(2)]
+    parts = (pl.ds(0, 3 * TOK // 4), pl.ds(3 * TOK // 4, TOK // 4))
+    x_cp = [[remote(tokbuf.at[m, OWN, part], tokbuf.at[m, XP, part], tx_s.at[m, k], tx_r.at[m, k], x_peer) for k, part in enumerate(parts)] for m in range(2)]
+    d_cp = [[remote(tokbuf.at[m, XP, part], tokbuf.at[m, DG, part], td_s.at[m, k], td_r.at[m, k], core_peer) for k, part in enumerate(parts)] for m in range(2)]
+    c_cp = [remote(tokbuf.at[m, OWN], tokbuf.at[m, CP], tc_s.at[m], tc_r.at[m], core_peer) for m in range(2)]
     for cp in (*xmeta_cp[0], *xmeta_cp[1], *cmeta_cp[0], *cmeta_cp[1], *x_cp[0], *c_cp):
         cp.start()
     local13 = (pltpu.make_async_copy(sw1, w13.at[SLOTS13 - 1, 0], w13_s.at[SLOTS13 - 1, 0]),
@@ -113,18 +116,16 @@
     for unit in range(SLOTS2):
         w2_copy(jnp.int32(unit)).start()
 
-    for cp in own_cp:
-        cp.wait()
-
     def route(i, carry):
         m, src = carry, i
-        first = ep * EXP + lax.broadcasted_iota(jnp.int32, (EXP, TOK), 0)
-        id_rows, slot_rows, gate_rows = ids[src, m, 0], ids[src, m, 1], gates[src, m]
+        first = (ep * EXP + lax.broadcasted_iota(jnp.int32, (EXP, TOK), 0)) * CAP
+        row_rows, gate_rows = ids[src, m], gates[src, m]
         slot = jnp.full((EXP, TOK), -1, jnp.int32)
         gate = jnp.zeros((EXP, TOK), F32)
         for j in range(TOP_K):
-            hit = (id_rows[j:j + 1, :] == first) & (slot_rows[j:j + 1, :] >= 0)
-            slot = jnp.where(hit, slot_rows[j:j + 1, :], slot)
+            place = row_rows[j:j + 1, :] - first
+            hit = (place >= 0) & (place < CAP)
+            slot = jnp.where(hit, place, slot)
             gate = jnp.where(hit, gate_rows[j:j + 1, :], gate)
         pos = lax.broadcasted_iota(jnp.int32, (CAP, TOK), 0)
         for e in range(EXP):
@@ -447,7 +448,8 @@
             in_specs=[hbm] * 14,
             out_specs=(vmem,) * 2 + (hbm,) * 3,
             scratch_shapes=[
-                pltpu.VMEM((NSRC, 2, 2, TOP_K, TOK), jnp.int32),
+                pltpu.VMEM((2, 2, TOP_K, TOK), jnp.int32),
+                pltpu.VMEM((NSRC, 2, TOP_K, TOK), jnp.int32),
                 pltpu.VMEM((NSRC, 2, TOP_K, TOK), F32),
                 pltpu.VMEM((2, NSRC, TOK, D), BF16),
                 pltpu.VMEM((2, NSRC, EXP, 1, TOK), jnp.int32),
@@ -463,7 +465,7 @@
                 pltpu.VMEM((steps, TOK, COL), F32),
                 pltpu.VMEM((SLOTS13, 2, D, F), BF16),
                 pltpu.VMEM((SLOTS2, PER, F, COL), BF16),
-                sem((2, 4)), sem((2, 2, 3)), sem((2, 2, 3)), sem((2, 3)), sem((2, 3)), sem((2,)), sem((2,)), sem((2, 2)), sem((2, 2)), sem((2, 2)), sem((2, 2)),
+                sem((2, 4)), sem((2, 2, 2)), sem((2, 2, 2)), sem((2, 2)), sem((2, 2)), sem((2,)), sem((2,)), sem((2, 2)), sem((2, 2)), sem((2, 2)), sem((2, 2)),
                 sem((4,)), sem((steps,)), sem((2,)), sem((steps,)), sem((steps,)), sem((steps,)),
                 sem((3,)), sem((3,)), sem((3,)), sem((3,)), sem((SLOTS13, 2)), sem((SLOTS2,)), sem((NCOL, 2)),
             ],

time: 109 us -> 108 us (level)
  no operation moved by 1% of the time
where the time goes in v5:
time: 108 us
  Pallas kernels  107 us (99%)
    pallas_call x1, Pallas kernels, layer_local(): pl.pallas_call(kernel, name='moe_layer', out_shape=(pltpu.VMEM((TOK, D),...  106 us

profile of v5, /device:TPU:0, one launch (start us, length us, event | category | flops | bytes accessed | tf_op | source)
XLA Modules:
  0.0 108.0 jit_solution(8378344844000233702)
XLA Ops:
  0.6 106.2 %moe_layer.1 = (bf16[256,1280]{1,0:T(8,128)(2,1)S(1)}, bf16[256,1280]{1,0:T(8,128)(2,1)S(1)}, bf16[1280,896]{1,0:T(8,128)(2,1)}, bf16[1280,896]{1,0:T(8,128)(2,1)}, bf16[896,1280]{1,0:T(8,128)(2,1)}) custom-call(bf16[256,1280]{1,0:T(8,128)(2,1)} %xa.1, bf16[256,1280]{1,0:T(8,128)(2,1)} %xb.1, s32[6,256]{1,0:T(8,128)} %bitcast.6, s32[6,256]{1,0:T(8,128)} %bitcast.7, ...), custom_call_target="tpu_custom_call" | custom-call | tf_op jit(solution)/shard_map/moe_layer/pallas_call | solution.py:444
  106.8 1.1 hand_over.1

commit v6 on v5

--- a/solution.py
+++ b/solution.py
@@ -90,7 +90,7 @@
     cmeta_cp = [[routing_cp(m, k, routing_slots(m, OWN), CP, meta_s.at[0], meta_r.at[0], core_peer) for k in range(2)] for m in range(2)]
     xmeta_cp = [[routing_cp(m, k, routing_slots(m, OWN), XP, meta_s.at[1], meta_r.at[1], x_peer) for k in range(2)] for m in range(2)]
     dmeta_cp = [[routing_cp(m, k, routing_slots(m, XP), DG, fmeta_s, fmeta_r, core_peer) for k in range(2)] for m in range(2)]
-    parts = (pl.ds(0, 3 * TOK // 4), pl.ds(3 * TOK // 4, TOK // 4))
+    parts = (pl.ds(0, 7 * TOK // 8), pl.ds(7 * TOK // 8, TOK // 8))
     x_cp = [[remote(tokbuf.at[m, OWN, part], tokbuf.at[m, XP, part], tx_s.at[m, k], tx_r.at[m, k], x_peer) for k, part in enumerate(parts)] for m in range(2)]
     d_cp = [[remote(tokbuf.at[m, XP, part], tokbuf.at[m, DG, part], td_s.at[m, k], td_r.at[m, k], core_peer) for k, part in enumerate(parts)] for m in range(2)]
     c_cp = [remote(tokbuf.at[m, OWN], tokbuf.at[m, CP], tc_s.at[m], tc_r.at[m], core_peer) for m in range(2)]
@@ -349,9 +349,10 @@
     def sw2_slot(half, n):
         return w13.at[2 + half, lax.div(n, 3), pl.ds(0, F), pl.ds(pl.multiple_of(lax.rem(n, 3) * COL, COL), COL)]
 
-    def sw2_copy(half, n):
-        return pltpu.make_async_copy((sw2, pw2)[half].at[:, pl.ds(pl.multiple_of(n * COL, COL), COL)], sw2_slot(half, n), sw2_s.at[n, half])
-
+    def sw2_copies(half):
+        return [pltpu.make_async_copy((sw2, pw2)[half].at[:, pl.ds(3 * k * COL, width)],
+                                      w13.at[2 + half, k, pl.ds(0, F), pl.ds(0, width)], sw2_s.at[half, k])
+                for k, width in enumerate((3 * COL, (NCOL - 3) * COL))]
 
     def fetch_peer(n):
         for i in range(2):
@@ -366,11 +367,11 @@
             fw_cp[2].start()
 
     far(1, fetch_peer)
-    for n in range(NCOL):
-        sw2_copy(0, jnp.int32(n)).start()
+    for cp in sw2_copies(0):
+        cp.start()
     fw_cp[2].wait()
-    for n in range(NCOL):
-        sw2_copy(1, jnp.int32(n)).start()
+    for cp in sw2_copies(1):
+        cp.start()
     for cp in peer13:
         cp.wait()
     shared_in(1, 1)
@@ -390,9 +391,10 @@
     for n in range(NCOL):
         far_copies(jnp.int32(n))[1].wait_send()
 
+    for cp in (*sw2_copies(0), *sw2_copies(1)):
+        cp.wait()
+
     def near_column(n, carry, refills=BLOCKS, final=False):
-        for half in range(2):
-            sw2_copy(half, n).wait()
         expand(2 * NCOL + n, hnear, NSRC, refills=refills)
         base = 2 * lax.rem(n, 2)
         cols = pl.ds(pl.multiple_of(n * COL, COL), COL)
@@ -467,7 +469,7 @@
                 pltpu.VMEM((SLOTS2, PER, F, COL), BF16),
                 sem((2, 4)), sem((2, 2, 2)), sem((2, 2, 2)), sem((2, 2)), sem((2, 2)), sem((2,)), sem((2,)), sem((2, 2)), sem((2, 2)), sem((2, 2)), sem((2, 2)),
                 sem((4,)), sem((steps,)), sem((2,)), sem((steps,)), sem((steps,)), sem((steps,)),
-                sem((3,)), sem((3,)), sem((3,)), sem((3,)), sem((SLOTS13, 2)), sem((SLOTS2,)), sem((NCOL, 2)),
+                sem((3,)), sem((3,)), sem((3,)), sem((3,)), sem((SLOTS13, 2)), sem((SLOTS2,)), sem((2, 2)),
             ],
             compiler_params=pltpu.CompilerParams(collective_id=0, has_side_effects=True, vmem_limit_bytes=67043328 - 1376256),
         )(tokens_a, tokens_b, experts_a.T, experts_b.T, gates_a.T, gates_b.T, slots_a.T, slots_b.T,

time: 108 us -> 108 us (level)
  no operation moved by 1% of the time
where the time goes in v6:
time: 108 us
  Pallas kernels  107 us (99%)
    pallas_call x1, Pallas kernels, layer_local(): pl.pallas_call(kernel, name='moe_layer', out_shape=(pltpu.VMEM((TOK, D),...  106 us

profile of v6, /device:TPU:0, one launch (start us, length us, event | category | flops | bytes accessed | tf_op | source)
XLA Modules:
  0.0 108.2 jit_solution(10247211872581063506)
XLA Ops:
  0.6 106.3 %moe_layer.1 = (bf16[256,1280]{1,0:T(8,128)(2,1)S(1)}, bf16[256,1280]{1,0:T(8,128)(2,1)S(1)}, bf16[1280,896]{1,0:T(8,128)(2,1)}, bf16[1280,896]{1,0:T(8,128)(2,1)}, bf16[896,1280]{1,0:T(8,128)(2,1)}) custom-call(bf16[256,1280]{1,0:T(8,128)(2,1)} %xa.1, bf16[256,1280]{1,0:T(8,128)(2,1)} %xb.1, s32[6,256]{1,0:T(8,128)} %bitcast.6, s32[6,256]{1,0:T(8,128)} %bitcast.7, ...), custom_call_target="tpu_custom_call" | custom-call | tf_op jit(solution)/shard_map/moe_layer/pallas_call | solution.py:446
  106.9 1.1 hand_over.1
